TPU v7x, 256 devices: a whole 4x4x8 slice. The times are simulated.
256 devices in a mesh: grp: 2 (over y_lo), row: 4 (over y_hi, core), col: 32 (over z, x).
Axes of the slice: x: 4, y: 4 (y_hi: 2, y_lo: 2; y = y_hi * 2 + y_lo), z: 8, core: 2. Of those that a mesh axis runs over, the one named last changes fastest.
Arguments:
- excitation: bfloat16 [2, 16, 32768], P('grp', None, ('row', 'col')), may hold values from -6 to 6
- panel_points: float32 [3, 32768], replicated, may hold values from 0 to 1
- panel_areas: float32 [32768], replicated, may hold values from 0.0027621358 to 0.011048543
- panel_map: int32 [32768], P(('row', 'col')), may hold values from 0 to 3
- interior_inverse: bfloat16 [32, 1024, 4, 2048], P('col', None, 'row'), may hold values from -0.0625 to 0.0625
- row_scales: float32 [32, 1024], P('col'), may hold values from 0.5 to 2
- iface_slot: int32 [32768], P(('row', 'col')), may hold values from 0 to 1
- iface_offset: int32 [32768], P(('row', 'col')), may hold values from 0 to 2047
- adjacency: int32 [4, 2], replicated, may hold values from 0 to 3, as said below
Outputs:
- traces: float32 [2, 16, 32768], P('grp', None, ('row', 'col'))
Inputs may be any that keep to these rules, and one draw needn't show every extreme that they name: `adjacency`: each row lists 2 different subdomains, none equal to the row's own index.
All inputs are finite; a program needn't handle non-finite values.
Results may differ from a plain program's by a relative error of at most 0.0015.
Values may be sent and summed in bfloat16 or wider, within the bound.
A program may use at most 128 MiB of HBM per device.

v0:
```python
import math

import jax
import jax.numpy as jnp
from jax import lax
from jax.sharding import PartitionSpec as P

ITERS = 4


robin_weight = 0.5
iface_weight = 0.4
wave_number = 40.0
soften = 0.05
self_term = 0.5


def partner(block, axis, bit):
    count = lax.axis_size(axis)
    route = []
    for low in range(count):
        high = low | 1 << bit
        if high != low and high < count:
            route += [(low, high), (high, low)]
    return lax.ppermute(block, axis, route)


def from_everyone(shard, axis):
    peers = lax.axis_size(axis)
    return lax.all_to_all(
        jnp.broadcast_to(shard[None], (peers, *shard.shape)), axis, 0, 0, tiled=True
    )


def laid_out(parts, dim):
    parts = jnp.moveaxis(parts, 0, dim)
    lengths = parts.shape
    return parts.reshape(*lengths[:dim], lengths[dim] * lengths[dim + 1], *lengths[dim + 2 :])


def collect(shard, axis, dim):
    parts = from_everyone(shard, axis)
    return laid_out(parts, dim)


def in_blocks(shard, dim, peers):
    lengths = shard.shape
    parts = shard.reshape(*lengths[:dim], peers, lengths[dim] // peers, *lengths[dim + 1 :])
    return jnp.moveaxis(parts, dim, 0)


def summed_on_arrival(shard, axis, dim):
    parts = in_blocks(shard, dim, lax.axis_size(axis))
    arrived = lax.all_to_all(parts, axis, split_axis=0, concat_axis=0, tiled=True)
    return arrived.sum(axis=0)


def kernel_block(panel_points, panel_areas, row_ids, col_start, count):
    row_points = jnp.take(panel_points, row_ids, axis=1)
    col_points = lax.dynamic_slice_in_dim(panel_points, col_start, count, 1)
    col_areas = lax.dynamic_slice_in_dim(panel_areas, col_start, count, 0)
    square = (row_points[0][:, None] - col_points[0][None, :]) ** 2
    square = square + (row_points[1][:, None] - col_points[1][None, :]) ** 2
    square = square + (row_points[2][:, None] - col_points[2][None, :]) ** 2
    distance = jnp.sqrt(square)
    return (col_areas[None, :] * jnp.cos(wave_number * distance) / (distance + soften)).astype(
        jnp.bfloat16
    )


def neighbour_of(adjacency, subdomain, slot):
    flat = adjacency.reshape(-1)
    wanted = subdomain * adjacency.shape[1] + slot
    hits = wanted[:, None] == jnp.arange(flat.shape[0], dtype=jnp.int32)[None, :]
    return jnp.sum(jnp.where(hits, flat[None, :], 0), axis=1)


def mix_both(
    base_outer,
    base_inner,
    outer_trace,
    inner_trace,
    inner_block,
    panel_map,
    iface_slot,
    iface_offset,
    adjacency,
    spots,
    sub_width,
):
    outer_index = panel_map * sub_width + spots % sub_width
    partner_sub = neighbour_of(adjacency, spots // sub_width, iface_slot)
    inner_index = partner_sub * sub_width + iface_offset
    far_inner = jnp.take(inner_block, outer_index, axis=1).astype(jnp.float32)
    near_inner = jnp.take(inner_block, inner_index, axis=1).astype(jnp.float32)
    outer_value = outer_trace.astype(jnp.float32)
    inner_value = inner_trace.astype(jnp.float32)
    mixed_outer = base_outer.astype(jnp.float32) + robin_weight * (far_inner - outer_value)
    mixed_inner = (
        base_inner.astype(jnp.float32)
        + robin_weight * (outer_value - inner_value)
        + iface_weight * (near_inner - inner_value)
    )
    return (mixed_outer.astype(jnp.bfloat16), mixed_inner.astype(jnp.bfloat16))


def body(
    excitation,
    panel_points,
    panel_areas,
    panel_map,
    interior_inverse,
    row_scales,
    iface_slot,
    iface_offset,
    adjacency,
):
    group = lax.axis_index("grp")
    row_index = lax.axis_index("row")
    column = lax.axis_index("col")
    strips = lax.axis_size("col")
    row_count = lax.axis_size("row")
    excitations = excitation.shape[1]
    piece = excitation.shape[2]
    sub_width = interior_inverse.shape[3]
    per_sub = sub_width // piece
    block = strips * piece
    tall = row_count * piece
    width = math.gcd(block, 1024)
    block_count = block // width
    base = excitation[0]
    own_spots = column * piece + jnp.arange(piece, dtype=jnp.int32)
    tile_rows = (
        jnp.arange(row_count, dtype=jnp.int32)[:, None] * block
        + column * piece
        + jnp.arange(piece, dtype=jnp.int32)[None, :]
    ).reshape(-1)
    col_start = row_index * block
    inverse_tile = interior_inverse[0, :, 0, :]
    scales_own = lax.dynamic_slice_in_dim(row_scales[0], row_index * piece, piece, 0)
    subdomain = column // per_sub

    def make_tiles(first, count, padded):

        def one_tile(index):
            return kernel_block(
                panel_points, panel_areas, tile_rows, col_start + (first + index) * width, width
            )

        made = lax.map(one_tile, jnp.arange(count, dtype=jnp.int32))
        return jnp.concatenate(
            [made, jnp.zeros((padded - count, tall, width), jnp.bfloat16)], axis=0
        )

    kept_tiles = lax.cond(
        group == 0,
        lambda operand: make_tiles(0, block_count, block_count),
        lambda operand: jnp.zeros((block_count, tall, width), jnp.bfloat16),
        0,
    )

    def exterior_range(mixed_block, count):
        columns = mixed_block.reshape(excitations, count, width)
        return lax.dot_general(
            columns, kept_tiles, (((1, 2), (0, 2)), ((), ())), preferred_element_type=jnp.float32
        )

    def interior_far(mixed_block):
        columns = lax.dynamic_slice_in_dim(mixed_block, subdomain * sub_width, sub_width, 1)
        return lax.dot_general(
            columns, inverse_tile, (((1,), (1,)), ((), ())), preferred_element_type=jnp.float32
        )

    state = jnp.zeros((excitations, piece), jnp.float32)
    for step in range(ITERS):
        trace = lax.optimization_barrier(state.astype(jnp.bfloat16))
        across = partner(trace, "grp", 0)
        outer_trace = jnp.where(group == 0, trace, across)
        inner_trace = jnp.where(group == 0, across, trace)
        inner_block = collect(inner_trace, "col", 1)
        outer_piece, inner_piece = mix_both(
            base,
            base,
            outer_trace,
            inner_trace,
            inner_block,
            panel_map,
            iface_slot,
            iface_offset,
            adjacency,
            own_spots,
            sub_width,
        )
        mixed = jnp.where(group == 0, outer_piece, inner_piece)
        mixed_block = collect(mixed, "col", 1)
        partial_rows = lax.cond(
            group == 0,
            lambda blocks: exterior_range(blocks, block_count),
            interior_far,
            mixed_block,
        )
        summed = summed_on_arrival(partial_rows, "row", 1)
        state = jnp.where(
            group == 0, self_term * mixed.astype(jnp.float32) + summed, scales_own[None, :] * summed
        )
    return state[None]


def solution(mesh):
    placed = (
        P("grp", None, ("row", "col")),
        P(),
        P(),
        P(("row", "col")),
        P("col", None, "row", None),
        P("col", None),
        P(("row", "col")),
        P(("row", "col")),
        P(),
    )
    return jax.shard_map(
        body, mesh=mesh, in_specs=placed, out_specs=P("grp", None, ("row", "col")), check_vma=False
    )
```

profile of v0, /device:TPU:1, one launch (start us, length us, event | category | flops | bytes accessed | tf_op | source)
XLA Modules:
  0.0 497.1 jit_solution(2425023701363038804)
XLA Ops:
  0.0 2.2 collective-permute-start
  4.5 11.0 %all-to-all-start = ((bf16[32,16,256]{2,1,0:T(8,128)(2,1)}), bf16[32,16,256]{2,1,0:T(8,128)(2,1)S(1)}, u32[]{:S(2)}, u32[]{:S(2)}) async-start(bf16[32,16,256]{2,1,0:T(8,128)(2,1)} %broadcast_in_dim.66), calls=%async_computation | async-start | bytes 524288 | tf_op jit(solution)/shard_map/all_to_all | solution.py:30
  16.3 9.6 %all-to-all-done = bf16[32,16,256]{2,1,0:T(8,128)(2,1)S(1)} async-done(((bf16[32,16,256]{2,1,0:T(8,128)(2,1)}), bf16[32,16,256]{2,1,0:T(8,128)(2,1)S(1)}, u32[]{:S(2)}, u32[]{:S(2)}) %all-to-all-start) | async-done | bytes 262176 | tf_op jit(solution)/shard_map/all_to_all | solution.py:30
  25.9 1.0 copy.180
  26.9 0.9 gather_fusion.1
  27.9 0.9 gather_fusion.2
  30.2 4.9 all-to-all-start.1
  35.2 265.4 %conditional.5 = (bf16[8,1024,1024]{2,1,0:T(8,128)(2,1)}) conditional(s32[]{:T(128)} %convert_element_type.136, () %tuple.45, (s32[]{:T(128)}, s32[4,1]{0,1:T(1,128)S(1)}, s32[]{:T(128)}, s32[4,256]{1,0:T(4,128)S(1)}, f32[32768]{0:T(1024)}, /*index=5*/f32[3,32768]{1,0:T(4,128)S(1)}) %tuple.138), branch_computations={%region_1.3_spmd, %region_2.6_spmd} | conditional | flops 13645842 | bytes 16777226 | solution.py:155
  35.2 8.6 %copy.184 = f32[3,32768]{0,1:T(8,128)} copy(f32[3,32768]{1,0:T(4,128)S(1)} %get-tuple-element.263) | data formatting | bytes 786432 | tf_op jit(solution)/shard_map
  43.9 256.7 %while.12 = (s32[]{:T(128)}, bf16[8,1024,1024]{2,1,0:T(8,128)(2,1)}, s32[8]{0:T(128)S(1)}, s32[]{:T(128)}, f32[32768]{0:T(1024)}, /*index=5*/s32[1024]{0:T(1024)...) while((s32[]{:T(128)}, ...), condition=%wide.region_4.5_spmd, body=%wide.region_3.4_spmd.sunk | while | flops 13644809 | bytes 2259691 | solution.py:150
  45.2 8.6 %gather_fusion = f32[1024,3]{1,0:T(8,128)S(1)} fusion(f32[3,32768]{0,1:T(8,128)} %get-tuple-element.400, s32[1024]{0:T(1024)S(1)} %broadcast_clamp_fusion.2), kind=kCustom, calls=%fused_computation.1.clone.1 | custom fusion | bytes 28672 | tf_op jit(solution)/shard_map/cond/branch_1_fun/while/body/eval_jaxpr/jit(_take)/gather | solution.py:59
  54.0 2.9 dynamic-slice_reduce_fusion.4
  57.6 18.3 %fusion.56 = bf16[8,1024,1024]{2,1,0:T(8,128)(2,1)} fusion(bf16[8,1024,1024]{2,1,0:T(8,128)(2,1)} %get-tuple-element.382, s32[]{:T(128)} %get-tuple-element.381, f32[1024]{0:T(1024)S(1)} %get-tuple-element.362, f32[1024]{0:T(1024)S(1)} %get-tuple-element.363, f32[1024]{0:T(1024)S(1)} %get-tuple-element.364, f32[1024]{0:T(1024)S(1)} %get-tuple-element.365, ...), kind=kLoop, calls=%fused_computation.30.clone.1 | loop fusion | flops 13631488 | bytes 2126336 | tf_op jit(solution)/shard_map/cond/branch_1_fun/while/body/jit(dynamic_update_index_in_dim)/dynamic_update_slice | solution.py:150
  77.2 8.6 %gather_fusion = f32[1024,3]{1,0:T(8,128)S(1)} fusion(f32[3,32768]{0,1:T(8,128)} %get-tuple-element.400, s32[1024]{0:T(1024)S(1)} %broadcast_clamp_fusion.2), kind=kCustom, calls=%fused_computation.1.clone.1 | custom fusion | bytes 28672 | tf_op jit(solution)/shard_map/cond/branch_1_fun/while/body/eval_jaxpr/jit(_take)/gather | solution.py:59
  86.0 3.0 dynamic-slice_reduce_fusion.4
  89.7 18.3 %fusion.56 = bf16[8,1024,1024]{2,1,0:T(8,128)(2,1)} fusion(bf16[8,1024,1024]{2,1,0:T(8,128)(2,1)} %get-tuple-element.382, s32[]{:T(128)} %get-tuple-element.381, f32[1024]{0:T(1024)S(1)} %get-tuple-element.362, f32[1024]{0:T(1024)S(1)} %get-tuple-element.363, f32[1024]{0:T(1024)S(1)} %get-tuple-element.364, f32[1024]{0:T(1024)S(1)} %get-tuple-element.365, ...), kind=kLoop, calls=%fused_computation.30.clone.1 | loop fusion | flops 13631488 | bytes 2126336 | tf_op jit(solution)/shard_map/cond/branch_1_fun/while/body/jit(dynamic_update_index_in_dim)/dynamic_update_slice | solution.py:150
  109.3 8.6 %gather_fusion = f32[1024,3]{1,0:T(8,128)S(1)} fusion(f32[3,32768]{0,1:T(8,128)} %get-tuple-element.400, s32[1024]{0:T(1024)S(1)} %broadcast_clamp_fusion.2), kind=kCustom, calls=%fused_computation.1.clone.1 | custom fusion | bytes 28672 | tf_op jit(solution)/shard_map/cond/branch_1_fun/while/body/eval_jaxpr/jit(_take)/gather | solution.py:59
  118.1 2.9 dynamic-slice_reduce_fusion.4
  121.6 18.3 %fusion.56 = bf16[8,1024,1024]{2,1,0:T(8,128)(2,1)} fusion(bf16[8,1024,1024]{2,1,0:T(8,128)(2,1)} %get-tuple-element.382, s32[]{:T(128)} %get-tuple-element.381, f32[1024]{0:T(1024)S(1)} %get-tuple-element.362, f32[1024]{0:T(1024)S(1)} %get-tuple-element.363, f32[1024]{0:T(1024)S(1)} %get-tuple-element.364, f32[1024]{0:T(1024)S(1)} %get-tuple-element.365, ...), kind=kLoop, calls=%fused_computation.30.clone.1 | loop fusion | flops 13631488 | bytes 2126336 | tf_op jit(solution)/shard_map/cond/branch_1_fun/while/body/jit(dynamic_update_index_in_dim)/dynamic_update_slice | solution.py:150
  141.3 8.6 %gather_fusion = f32[1024,3]{1,0:T(8,128)S(1)} fusion(f32[3,32768]{0,1:T(8,128)} %get-tuple-element.400, s32[1024]{0:T(1024)S(1)} %broadcast_clamp_fusion.2), kind=kCustom, calls=%fused_computation.1.clone.1 | custom fusion | bytes 28672 | tf_op jit(solution)/shard_map/cond/branch_1_fun/while/body/eval_jaxpr/jit(_take)/gather | solution.py:59
  150.1 3.0 dynamic-slice_reduce_fusion.4
  153.7 18.3 %fusion.56 = bf16[8,1024,1024]{2,1,0:T(8,128)(2,1)} fusion(bf16[8,1024,1024]{2,1,0:T(8,128)(2,1)} %get-tuple-element.382, s32[]{:T(128)} %get-tuple-element.381, f32[1024]{0:T(1024)S(1)} %get-tuple-element.362, f32[1024]{0:T(1024)S(1)} %get-tuple-element.363, f32[1024]{0:T(1024)S(1)} %get-tuple-element.364, f32[1024]{0:T(1024)S(1)} %get-tuple-element.365, ...), kind=kLoop, calls=%fused_computation.30.clone.1 | loop fusion | flops 13631488 | bytes 2126336 | tf_op jit(solution)/shard_map/cond/branch_1_fun/while/body/jit(dynamic_update_index_in_dim)/dynamic_update_slice | solution.py:150
  173.4 8.6 %gather_fusion = f32[1024,3]{1,0:T(8,128)S(1)} fusion(f32[3,32768]{0,1:T(8,128)} %get-tuple-element.400, s32[1024]{0:T(1024)S(1)} %broadcast_clamp_fusion.2), kind=kCustom, calls=%fused_computation.1.clone.1 | custom fusion | bytes 28672 | tf_op jit(solution)/shard_map/cond/branch_1_fun/while/body/eval_jaxpr/jit(_take)/gather | solution.py:59
  182.2 3.0 dynamic-slice_reduce_fusion.4
  185.8 18.3 %fusion.56 = bf16[8,1024,1024]{2,1,0:T(8,128)(2,1)} fusion(bf16[8,1024,1024]{2,1,0:T(8,128)(2,1)} %get-tuple-element.382, s32[]{:T(128)} %get-tuple-element.381, f32[1024]{0:T(1024)S(1)} %get-tuple-element.362, f32[1024]{0:T(1024)S(1)} %get-tuple-element.363, f32[1024]{0:T(1024)S(1)} %get-tuple-element.364, f32[1024]{0:T(1024)S(1)} %get-tuple-element.365, ...), kind=kLoop, calls=%fused_computation.30.clone.1 | loop fusion | flops 13631488 | bytes 2126336 | tf_op jit(solution)/shard_map/cond/branch_1_fun/while/body/jit(dynamic_update_index_in_dim)/dynamic_update_slice | solution.py:150
  205.5 8.6 %gather_fusion = f32[1024,3]{1,0:T(8,128)S(1)} fusion(f32[3,32768]{0,1:T(8,128)} %get-tuple-element.400, s32[1024]{0:T(1024)S(1)} %broadcast_clamp_fusion.2), kind=kCustom, calls=%fused_computation.1.clone.1 | custom fusion | bytes 28672 | tf_op jit(solution)/shard_map/cond/branch_1_fun/while/body/eval_jaxpr/jit(_take)/gather | solution.py:59
  214.3 3.2 dynamic-slice_reduce_fusion.4
  218.1 18.3 %fusion.56 = bf16[8,1024,1024]{2,1,0:T(8,128)(2,1)} fusion(bf16[8,1024,1024]{2,1,0:T(8,128)(2,1)} %get-tuple-element.382, s32[]{:T(128)} %get-tuple-element.381, f32[1024]{0:T(1024)S(1)} %get-tuple-element.362, f32[1024]{0:T(1024)S(1)} %get-tuple-element.363, f32[1024]{0:T(1024)S(1)} %get-tuple-element.364, f32[1024]{0:T(1024)S(1)} %get-tuple-element.365, ...), kind=kLoop, calls=%fused_computation.30.clone.1 | loop fusion | flops 13631488 | bytes 2126336 | tf_op jit(solution)/shard_map/cond/branch_1_fun/while/body/jit(dynamic_update_index_in_dim)/dynamic_update_slice | solution.py:150
  237.7 8.6 %gather_fusion = f32[1024,3]{1,0:T(8,128)S(1)} fusion(f32[3,32768]{0,1:T(8,128)} %get-tuple-element.400, s32[1024]{0:T(1024)S(1)} %broadcast_clamp_fusion.2), kind=kCustom, calls=%fused_computation.1.clone.1 | custom fusion | bytes 28672 | tf_op jit(solution)/shard_map/cond/branch_1_fun/while/body/eval_jaxpr/jit(_take)/gather | solution.py:59
  246.5 3.0 dynamic-slice_reduce_fusion.4
  250.2 18.3 %fusion.56 = bf16[8,1024,1024]{2,1,0:T(8,128)(2,1)} fusion(bf16[8,1024,1024]{2,1,0:T(8,128)(2,1)} %get-tuple-element.382, s32[]{:T(128)} %get-tuple-element.381, f32[1024]{0:T(1024)S(1)} %get-tuple-element.362, f32[1024]{0:T(1024)S(1)} %get-tuple-element.363, f32[1024]{0:T(1024)S(1)} %get-tuple-element.364, f32[1024]{0:T(1024)S(1)} %get-tuple-element.365, ...), kind=kLoop, calls=%fused_computation.30.clone.1 | loop fusion | flops 13631488 | bytes 2126336 | tf_op jit(solution)/shard_map/cond/branch_1_fun/while/body/jit(dynamic_update_index_in_dim)/dynamic_update_slice | solution.py:150
  269.8 8.6 %gather_fusion = f32[1024,3]{1,0:T(8,128)S(1)} fusion(f32[3,32768]{0,1:T(8,128)} %get-tuple-element.400, s32[1024]{0:T(1024)S(1)} %broadcast_clamp_fusion.2), kind=kCustom, calls=%fused_computation.1.clone.1 | custom fusion | bytes 28672 | tf_op jit(solution)/shard_map/cond/branch_1_fun/while/body/eval_jaxpr/jit(_take)/gather | solution.py:59
  278.6 3.0 dynamic-slice_reduce_fusion.4
  282.3 18.3 %fusion.56 = bf16[8,1024,1024]{2,1,0:T(8,128)(2,1)} fusion(bf16[8,1024,1024]{2,1,0:T(8,128)(2,1)} %get-tuple-element.382, s32[]{:T(128)} %get-tuple-element.381, f32[1024]{0:T(1024)S(1)} %get-tuple-element.362, f32[1024]{0:T(1024)S(1)} %get-tuple-element.363, f32[1024]{0:T(1024)S(1)} %get-tuple-element.364, f32[1024]{0:T(1024)S(1)} %get-tuple-element.365, ...), kind=kLoop, calls=%fused_computation.30.clone.1 | loop fusion | flops 13631488 | bytes 2126336 | tf_op jit(solution)/shard_map/cond/branch_1_fun/while/body/jit(dynamic_update_index_in_dim)/dynamic_update_slice | solution.py:150
  300.6 10.5 %conditional.6 = (f32[16,1024]{1,0:T(8,128)S(1)}) conditional(s32[]{:T(128)} %convert_element_type.136, (bf16[16,32,256]{2,0,1:T(8,128)(2,1)S(1)}, s32[]{:T(128)}, bf16[1024,2048]{1,0:T(8,128)(2,1)}) %tuple.130, (bf16[16,32,256]{2,0,1:T(8,128)(2,1)S(1)}, bf16[8,1024,1024]{2,1,0:T(8,128)(2,1)}) %tuple.131), branch_computations={%region_5.7_spmd, %region_6.8_spmd} | conditional | flops 268435456 | bytes 18153480 | solution.py:196
  300.9 10.3 %convolution_bitcast_fusion = f32[16,1024]{1,0:T(8,128)S(1)} fusion(bf16[8,1024,1024]{2,1,0:T(8,128)(2,1)} %get-tuple-element.148, bf16[16,8,1024]{2,1,0:T(8,128)(2,1)S(1)} %reshape_reshape.8), kind=kOutput, calls=%fused_computation.12 | convolution fusion | flops 268435456 | bytes 17104896 | tf_op jit(solution)/shard_map/cond/branch_1_fun/dot_general | solution.py:164
  311.8 6.5 %all-to-all-start.2 = ((f32[4,16,256]{2,1,0:T(8,128)}), f32[4,16,256]{2,1,0:T(8,128)S(1)}, u32[]{:S(2)}, u32[]{:S(2)}) async-start(f32[4,16,256]{2,1,0:T(8,128)} %copy.187), calls=%async_computation.2 | async-start | bytes 131072 | tf_op jit(solution)/shard_map/all_to_all | solution.py:54
  318.3 4.8 all-to-all-done.2
  323.2 2.5 collective-permute-done.1
  325.7 19.7 %all_to_all.60 = bf16[32,16,256]{2,1,0:T(8,128)(2,1)S(1)} all-to-all(bf16[32,16,256]{2,1,0:T(8,128)(2,1)S(1)} %broadcast_in_dim.118), channel_id=1, replica_groups=mesh['grp'=2,'row'=4,'col'=32] {'col'}, dimensions={0} | all-to-all | bytes 524288 | tf_op jit(solution)/shard_map/all_to_all | solution.py:30
  345.4 1.0 copy.189
  346.4 0.9 gather_fusion.3
  347.3 0.9 gather_fusion.4
  348.4 14.2 %all_to_all.61 = bf16[32,16,256]{2,1,0:T(8,128)(2,1)S(1)} all-to-all(bf16[32,16,256]{2,1,0:T(8,128)(2,1)S(1)} %broadcast_in_dim.119), channel_id=1, replica_groups=mesh['grp'=2,'row'=4,'col'=32] {'col'}, dimensions={0} | all-to-all | bytes 524288 | tf_op jit(solution)/shard_map/all_to_all | solution.py:30
  362.5 10.5 %conditional.7 = (f32[16,1024]{1,0:T(8,128)S(1)}) conditional(s32[]{:T(128)} %convert_element_type.136, (bf16[16,32,256]{2,0,1:T(8,128)(2,1)S(1)}, s32[]{:T(128)}, bf16[1024,2048]{1,0:T(8,128)(2,1)}) %tuple.134, (bf16[16,32,256]{2,0,1:T(8,128)(2,1)S(1)}, bf16[8,1024,1024]{2,1,0:T(8,128)(2,1)}) %tuple.135), branch_computations={%region_8.10_spmd, %region_9.11_spmd} | conditional | flops 268435456 | bytes 18153480 | solution.py:196
  362.8 10.3 %convolution_bitcast_fusion.1 = f32[16,1024]{1,0:T(8,128)S(1)} fusion(bf16[8,1024,1024]{2,1,0:T(8,128)(2,1)} %get-tuple-element.153, bf16[16,8,1024]{2,1,0:T(8,128)(2,1)S(1)} %reshape_reshape.9), kind=kOutput, calls=%fused_computation.17 | convolution fusion | flops 268435456 | bytes 17104896 | tf_op jit(solution)/shard_map/cond/branch_1_fun/dot_general | solution.py:164
  373.1 11.6 %all_to_all.62 = f32[4,16,256]{2,1,0:T(8,128)S(1)} all-to-all(f32[4,16,256]{2,1,0:T(8,128)S(1)} %copy.194), channel_id=1, replica_groups=mesh['grp'=2,'row'=4,'col'=32] {'row'}, dimensions={0} | all-to-all | bytes 131072 | tf_op jit(solution)/shard_map/all_to_all | solution.py:54
  384.9 2.5 collective-permute-done.2
  387.4 14.0 %all_to_all.63 = bf16[32,16,256]{2,1,0:T(8,128)(2,1)S(1)} all-to-all(bf16[32,16,256]{2,1,0:T(8,128)(2,1)S(1)} %broadcast_in_dim.120), channel_id=1, replica_groups=mesh['grp'=2,'row'=4,'col'=32] {'col'}, dimensions={0} | all-to-all | bytes 524288 | tf_op jit(solution)/shard_map/all_to_all | solution.py:30
  401.4 1.0 copy.196
  402.4 0.9 gather_fusion.5
  403.2 0.9 gather_fusion.6
  404.3 14.2 %all_to_all.64 = bf16[32,16,256]{2,1,0:T(8,128)(2,1)S(1)} all-to-all(bf16[32,16,256]{2,1,0:T(8,128)(2,1)S(1)} %broadcast_in_dim.121), channel_id=1, replica_groups=mesh['grp'=2,'row'=4,'col'=32] {'col'}, dimensions={0} | all-to-all | bytes 524288 | tf_op jit(solution)/shard_map/all_to_all | solution.py:30
  418.5 10.5 %conditional.8 = (f32[16,1024]{1,0:T(8,128)S(1)}) conditional(s32[]{:T(128)} %convert_element_type.136, (bf16[16,32,256]{2,0,1:T(8,128)(2,1)S(1)}, s32[]{:T(128)}, bf16[1024,2048]{1,0:T(8,128)(2,1)}) %tuple.136, (bf16[16,32,256]{2,0,1:T(8,128)(2,1)S(1)}, bf16[8,1024,1024]{2,1,0:T(8,128)(2,1)}) %tuple.137), branch_computations={%region_11.13_spmd, %region_12.14_spmd} | conditional | flops 268435456 | bytes 18153480 | solution.py:196
  418.7 10.3 %convolution_bitcast_fusion.2 = f32[16,1024]{1,0:T(8,128)S(1)} fusion(bf16[8,1024,1024]{2,1,0:T(8,128)(2,1)} %get-tuple-element.158, bf16[16,8,1024]{2,1,0:T(8,128)(2,1)S(1)} %reshape_reshape.10), kind=kOutput, calls=%fused_computation.22 | convolution fusion | flops 268435456 | bytes 17104896 | tf_op jit(solution)/shard_map/cond/branch_1_fun/dot_general | solution.py:164
  429.1 11.6 %all_to_all.65 = f32[4,16,256]{2,1,0:T(8,128)S(1)} all-to-all(f32[4,16,256]{2,1,0:T(8,128)S(1)} %copy.201), channel_id=1, replica_groups=mesh['grp'=2,'row'=4,'col'=32] {'row'}, dimensions={0} | all-to-all | bytes 131072 | tf_op jit(solution)/shard_map/all_to_all | solution.py:54
  440.8 2.5 collective-permute-done.3
  443.4 13.8 %all_to_all.66 = bf16[32,16,256]{2,1,0:T(8,128)(2,1)S(1)} all-to-all(bf16[32,16,256]{2,1,0:T(8,128)(2,1)S(1)} %broadcast_in_dim.122), channel_id=1, replica_groups=mesh['grp'=2,'row'=4,'col'=32] {'col'}, dimensions={0} | all-to-all | bytes 524288 | tf_op jit(solution)/shard_map/all_to_all | solution.py:30
  457.1 1.0 copy.203
  458.1 0.9 gather_fusion.7
  460.1 14.2 %all_to_all.67 = bf16[32,16,256]{2,1,0:T(8,128)(2,1)S(1)} all-to-all(bf16[32,16,256]{2,1,0:T(8,128)(2,1)S(1)} %broadcast_in_dim.123), channel_id=1, replica_groups=mesh['grp'=2,'row'=4,'col'=32] {'col'}, dimensions={0} | all-to-all | bytes 524288 | tf_op jit(solution)/shard_map/all_to_all | solution.py:30
  474.2 10.5 %conditional.9 = (f32[16,1024]{1,0:T(8,128)S(1)}) conditional(s32[]{:T(128)} %convert_element_type.136, (bf16[16,32,256]{2,0,1:T(8,128)(2,1)S(1)}, s32[]{:T(128)}, bf16[1024,2048]{1,0:T(8,128)(2,1)}) %tuple.132, (bf16[16,32,256]{2,0,1:T(8,128)(2,1)S(1)}, bf16[8,1024,1024]{2,1,0:T(8,128)(2,1)}) %tuple.133), branch_computations={%region_14.16_spmd, %region_15.17_spmd} | conditional | flops 268435456 | bytes 18153480 | solution.py:196
  474.5 10.3 %convolution_bitcast_fusion.3 = f32[16,1024]{1,0:T(8,128)S(1)} fusion(bf16[8,1024,1024]{2,1,0:T(8,128)(2,1)} %get-tuple-element.163, bf16[16,8,1024]{2,1,0:T(8,128)(2,1)S(1)} %reshape_reshape.11), kind=kOutput, calls=%fused_computation.27 | convolution fusion | flops 268435456 | bytes 17104896 | tf_op jit(solution)/shard_map/cond/branch_1_fun/dot_general | solution.py:164
  484.8 11.6 %all_to_all.68 = f32[4,16,256]{2,1,0:T(8,128)S(1)} all-to-all(f32[4,16,256]{2,1,0:T(8,128)S(1)} %copy.208), channel_id=1, replica_groups=mesh['grp'=2,'row'=4,'col'=32] {'row'}, dimensions={0} | all-to-all | bytes 131072 | tf_op jit(solution)/shard_map/all_to_all | solution.py:54
  (124 shorter events, 21.3 us)
Async XLA Ops:
  0.0 318.3 %copy-start = (f32[1,1024]{1,0:T(1,128)S(1)}, f32[1,1024]{1,0:T(1,128)}, u32[]{:S(2)}) copy-start(f32[1,1024]{1,0:T(1,128)} %param.28) | copy-start | bytes 12292
  0.0 35.2 %copy-start.1 = (f32[3,32768]{1,0:T(4,128)S(1)}, f32[3,32768]{1,0:T(4,128)}, u32[]{:S(2)}) copy-start(f32[3,32768]{1,0:T(4,128)} %param.24) | copy-start | bytes 1179652
  0.0 3.7 collective-permute-start
  4.5 21.4 %all-to-all-start = ((bf16[32,16,256]{2,1,0:T(8,128)(2,1)}), bf16[32,16,256]{2,1,0:T(8,128)(2,1)S(1)}, u32[]{:S(2)}, u32[]{:S(2)}) async-start(bf16[32,16,256]{2,1,0:T(8,128)(2,1)} %broadcast_in_dim.66), calls=%async_computation | async-start | bytes 524288 | tf_op jit(solution)/shard_map/all_to_all | solution.py:30
  30.2 270.4 %all-to-all-start.1 = ((bf16[32,16,256]{2,1,0:T(8,128)(2,1)}), bf16[32,16,256]{2,1,0:T(8,128)(2,1)S(1)}, u32[]{:S(2)}, u32[]{:S(2)}) async-start(bf16[32,16,256]{2,1,0:T(8,128)(2,1)} %broadcast_in_dim.70), calls=%async_computation.1 | async-start | bytes 524288 | tf_op jit(solution)/shard_map/all_to_all | solution.py:30
  300.6 47.7 %copy-start.2 = (bf16[1,16,256]{2,1,0:T(8,128)(2,1)S(1)}, bf16[1,16,256]{2,1,0:T(8,128)(2,1)}, u32[]{:S(2)}) copy-start(bf16[1,16,256]{2,1,0:T(8,128)(2,1)} %param.23) | copy-start | bytes 24580
  311.8 11.3 %all-to-all-start.2 = ((f32[4,16,256]{2,1,0:T(8,128)}), f32[4,16,256]{2,1,0:T(8,128)S(1)}, u32[]{:S(2)}, u32[]{:S(2)}) async-start(f32[4,16,256]{2,1,0:T(8,128)} %copy.187), calls=%async_computation.2 | async-start | bytes 131072 | tf_op jit(solution)/shard_map/all_to_all | solution.py:54
  323.1 2.6 collective-permute-start.1
  384.8 2.6 collective-permute-start.2
  440.7 2.6 collective-permute-start.3
where the time goes:
time: 499 us; the launch traced here: 497 us
  other arithmetic  152 us (30%)
  local copies, waits for them, and re-layouts  127 us (25%)
  blocking collectives  125 us (25%)
  matrix products  41 us (8%)
  starting transfers between devices  24.9 us (5%)
  waiting for transfers between devices  21.8 us (4%)
  loops' own time  5.61 us (1%)
    dynamic_update_slice x8, other arithmetic, make_tiles(): made = lax.map(one_tile, jnp.arange(count, dtype=jnp.int32))  147 us
    all_to_all x6, blocking collectives, from_everyone(): lax.all_to_all(jnp.broadcast_to(shard[None], (peers, *shard.shape)), axis...  89.9 us
    gather x8, local copies, waits for them, and re-layouts, kernel_block(): row_points = jnp.take(panel_points, row_ids, axis=1)  68.6 us
    dot_general x4, matrix products, exterior_range(): lax.dot_general(columns, kept_tiles, (((1, 2), (0, 2)), ((), ())), prefer...  41 us
    all_to_all x3, blocking collectives, summed_on_arrival(): lax.all_to_all(parts, axis, split_axis=0, concat_axis=0, tiled=True)  34.9 us
    slice x8, local copies, waits for them, and re-layouts, kernel_block(): square = (row_points[0][:, None] - col_points[0][None, :]) ** 2  23.8 us
    all_to_all x2, starting transfers between devices, from_everyone(): lax.all_to_all(jnp.broadcast_to(shard[None], (peers, *shard.shape)), axis...  15.9 us
  transfers between devices with their start and end apart: 7, of which 5 were waited for; matrix products, arithmetic and copies ran while one was open for 53% of the time, Pallas kernels for 0%

commit v1 on v0

v1 whole, which is shorter than its diff:
```python
import functools
import math

import jax
import jax.numpy as jnp
from jax import lax
from jax.experimental import pallas as pl
from jax.experimental.pallas import tpu as pltpu
from jax.sharding import PartitionSpec as P

ITERS = 4
GROUPS = 2
robin_weight = 0.5
iface_weight = 0.4
wave_number = 40.0
soften = 0.05
self_term = 0.5
KB = 32
X_CHIPS = 4

BF = jnp.bfloat16
F32 = jnp.float32
MESH = pl.DeviceIdType.MESH

COS_TERMS = (
    1.4142135381698608,
    -6.978850841522217,
    5.739460468292236,
    -1.883557915687561,
    0.3106880187988281,
)
TURNS = wave_number / (2.0 * math.pi)


def kernel(
    dims,
    exc,
    pts,
    areas,
    pmap,
    slot,
    off,
    adj,
    inv,
    scales,
    out,
    ipt,
    stage,
    kpt,
    kbuf,
    abuf,
    gbuf,
    metasend,
    metabuf,
    xmeta,
    bbuf,
    tsend,
    tbuf,
    we,
    nsend,
    nbuf,
    wi,
    acc,
    psend,
    pbuf,
    ubuf,
    asem,
    b_s,
    b_r,
    m_s,
    m_r,
    t_s,
    t_r,
    x_s,
    x_r,
    y_s,
    y_r,
):
    Z, X, R, piece, block = dims
    Zh = Z // GROUPS
    sub_width = GROUPS * X * piece
    RP = R * piece
    g = lax.axis_index("grp")
    r = lax.axis_index("row")
    c = lax.axis_index("col")
    z, x = c // X, c % X
    s = z // GROUPS
    zt = GROUPS * s + g
    parity = z % GROUPS
    me = g * R + r

    def remote(src, dst, ss, rs, dev):
        return pltpu.make_async_remote_copy(
            src_ref=src, dst_ref=dst, send_sem=ss, recv_sem=rs, device_id=dev, device_id_type=MESH
        )

    def col_of(zz, xx):
        return zz * X + xx

    barrier = pltpu.get_barrier_semaphore()
    n_partners = 0
    for flip in range(GROUPS):
        for dz in range(Z):
            if flip or dz:
                pl.semaphore_signal(
                    barrier,
                    inc=1,
                    device_id={"grp": (g + flip) % GROUPS, "row": r, "col": col_of((z + dz) % Z, x)},
                    device_id_type=MESH,
                )
                n_partners += 1
    for dx in range(1, X):
        pl.semaphore_signal(
            barrier,
            inc=1,
            device_id={"grp": g, "row": r, "col": col_of(z, (x + dx) % X)},
            device_id_type=MESH,
        )
        n_partners += 1
    for flip in range(GROUPS):
        for dr in range(1, R):
            pl.semaphore_signal(
                barrier,
                inc=1,
                device_id={"grp": (g + flip) % GROUPS, "row": (r + dr) % R, "col": c},
                device_id_type=MESH,
            )
            n_partners += 1

    inverse_copy = pltpu.make_async_copy(
        inv.at[:, pl.ds(pl.multiple_of(g * X * piece, X * piece), X * piece)], abuf, asem
    )
    inverse_copy.start()

    for rr in range(R):
        start = pl.multiple_of(rr * block + c * piece, piece)
        ipt[0:3, rr * piece : (rr + 1) * piece] = pts[:, pl.ds(start, piece)] * TURNS
    stage[...] = jnp.zeros_like(stage)

    def stage_points(p, carry):
        xx, zi = p // Zh, p % Zh
        start = pl.multiple_of(r * block + col_of(GROUPS * zi + g, xx) * piece, piece)
        stage[0:3, :] = pts[:, pl.ds(start, piece)] * TURNS
        stage[3:4, :] = areas[:, pl.ds(start, piece)] * TURNS
        kpt[pl.ds(pl.multiple_of(p * piece, piece), piece), :] = jnp.transpose(stage[...])
        return carry

    lax.fori_loop(0, X * Zh, stage_points, 0)

    per_piece = piece // KB

    def make_rows(t, carry):
        p = t // per_piece
        row = pl.multiple_of((t % per_piece) * KB, KB)
        kc = kpt[pl.ds(pl.multiple_of(t * KB, KB), KB), :]
        ix, iy, iz = ipt[0:1, :], ipt[1:2, :], ipt[2:3, :]
        dx = ix - kc[:, 0:1]
        dy = iy - kc[:, 1:2]
        dz = iz - kc[:, 2:3]
        square = dx * dx + dy * dy
        square = jnp.maximum(square + dz * dz, 1e-30)
        turns = square * lax.rsqrt(square)
        part = turns - jnp.round(turns)
        v = part * part
        h = COS_TERMS[4] * v + COS_TERMS[3]
        h = h * v + COS_TERMS[2]
        h = h * v + COS_TERMS[1]
        h = h * v + COS_TERMS[0]
        area = kc[:, 3:4]
        top = area * (h * h) - area
        value = top / (turns + soften * TURNS)
        kbuf[p // Zh, p % Zh, pl.ds(row, KB), :] = value.astype(BF)
        return carry

    quarter = X * Zh * per_piece // 4

    def make_quarter(q):
        lax.fori_loop(q * quarter, (q + 1) * quarter, make_rows, 0)

    make_quarter(0)
    pl.semaphore_wait(barrier, n_partners)

    metasend[...] = jnp.zeros_like(metasend)
    metasend[0:1, :] = pmap[...]
    metasend[1:2, :] = slot[...] * sub_width + off[...]
    b_plane = parity

    def b_copy(dz):
        return remote(
            exc.at[0],
            bbuf.at[g, z],
            b_s.at[dz],
            b_r.at[g, z],
            {"grp": b_plane, "row": r, "col": col_of((z + dz) % Z, x)},
        )

    def m_copy(dz):
        return remote(
            metasend,
            metabuf.at[z],
            m_s.at[dz],
            m_r.at[z],
            {"grp": g, "row": r, "col": col_of((z + dz) % Z, x)},
        )

    order = sorted(range(Z), key=lambda dz: -min(dz, Z - dz))
    for dz in order:
        if dz:
            b_copy(dz).start()

            @pl.when(b_plane == g)
            def _():
                m_copy(dz).start()
        else:

            @pl.when(b_plane != g)
            def _():
                b_copy(0).start()

            @pl.when(b_plane == g)
            def _():
                bbuf[g, z] = exc[0]
                metabuf[z] = metasend[...]

    make_quarter(1)

    for zi in range(Zh):
        zs = GROUPS * zi + g
        for src in range(GROUPS):

            @pl.when((zs != z) | (g != src))
            def _():
                remote(
                    bbuf.at[src, zs], bbuf.at[src, zs], b_s.at[0], b_r.at[src, zs], {"row": r}
                ).wait_recv()

        @pl.when(zs != z)
        def _():
            remote(metabuf.at[zs], metabuf.at[zs], m_s.at[0], m_r.at[zs], {"row": r}).wait_recv()

    def x_dev(dx):
        return {"grp": g, "row": r, "col": col_of(z, (x + dx) % X)}

    x_order = sorted(range(1, X), key=lambda dx: -min(dx, X - dx))

    def we_copy(k, dx):
        return remote(we.at[k, x], we.at[k, x], x_s.at[0, dx], x_r.at[k, 0, x], x_dev(dx))

    def n_copy(k, dx):
        return remote(
            nsend.at[k, (x + dx) % X], nbuf.at[k, x], x_s.at[1, dx], x_r.at[k, 1, x], x_dev(dx)
        )

    def wi_copy(k, dx):
        return remote(wi.at[k, x], wi.at[k, x], x_s.at[2, dx], x_r.at[k, 2, x], x_dev(dx))

    def xm_copy(dx):
        return remote(metabuf.at[zt], xmeta.at[x], x_s.at[1, dx], x_r.at[0, 1, x], x_dev(dx))

    def x_wait(ref, k, kind, dx):
        xs = (x + dx) % X
        remote(ref, ref, x_s.at[kind, dx], x_r.at[k, kind, xs], x_dev(dx)).wait_recv()

    for zi in range(Zh):
        we[0, x, zi] = bbuf[0, GROUPS * zi + g]
    wi[0, x] = bbuf[1, zt]
    xmeta[x] = metabuf[zt]
    for dx in x_order:
        we_copy(0, dx).start()
        xm_copy(dx).start()
        wi_copy(0, dx).start()
    make_quarter(2)

    for dx in range(1, X):
        xs = (x + dx) % X
        x_wait(xmeta.at[xs], 0, 1, dx)

    def make_gather(t, carry):
        xx, q = t // (GROUPS * GROUPS), t % (GROUPS * GROUPS)
        code = xmeta[xx, 1:2, :]
        src_x = (code // piece) % X
        src_q = code // (X * piece)
        here = jnp.where((src_x == x) & (src_q == q), code % piece, -1)
        rows = lax.broadcasted_iota(jnp.int32, (piece, piece), 0)
        hit = jnp.where(rows == here, 1.0, 0.0).astype(BF)
        gbuf[q, :, pl.ds(pl.multiple_of(xx * piece, piece), piece)] = hit
        return carry

    lax.fori_loop(0, X * GROUPS * GROUPS, make_gather, 0)
    make_quarter(3)
    inverse_copy.wait()
    for dx in range(1, X):
        x_wait(we.at[0, (x + dx) % X], 0, 0, dx)
        x_wait(wi.at[0, (x + dx) % X], 0, 2, dx)
        we_copy(0, dx).wait_send()
        xm_copy(dx).wait_send()
        wi_copy(0, dx).wait_send()
    for dz in order:
        if dz:
            b_copy(dz).wait_send()

            @pl.when(b_plane == g)
            def _():
                m_copy(dz).wait_send()
        else:

            @pl.when(b_plane != g)
            def _():
                b_copy(0).wait_send()

    def y_copy(k, kind, rr):
        return remote(
            psend.at[k, kind, rr],
            pbuf.at[k, me],
            y_s.at[kind, rr],
            y_r.at[k, me],
            {"grp": kind, "row": rr, "col": c},
        )

    def give(k, kind, rr, value):
        psend[k, kind, rr] = value
        own = (g == kind) & (r == rr)

        @pl.when(jnp.logical_not(own))
        def _():
            y_copy(k, kind, rr).start()

        @pl.when(own)
        def _():
            pbuf[k, me] = value

    def outer_part(k, xs, columns):
        total = None
        for zi in range(Zh):
            term = jnp.dot(we[k, xs, zi], kbuf[xs, zi, :, columns], preferred_element_type=F32)
            total = term if total is None else total + term
        return total

    everything = slice(None)

    def send_rows(k, xs):
        for j in range(R):
            rr = (r + 1 + j) % R
            columns = pl.ds(pl.multiple_of(rr * piece, piece), piece)
            value = acc[:, columns] + outer_part(k, xs, columns)
            own_piece = self_term * we[k, x, z // GROUPS].astype(F32)
            value = value + jnp.where((rr == r) & (parity == g), own_piece, 0.0)
            give(k, 0, rr, value)

    def inner_rows(k):
        for j in range(R):
            rr = (r + 1 + j) % R
            rows = pl.ds(pl.multiple_of(rr * piece, piece), piece)
            total = None
            for xx in range(X):
                term = lax.dot_general(
                    wi[k, xx],
                    abuf[rows, xx * piece : (xx + 1) * piece],
                    (((1,), (1,)), ((), ())),
                    preferred_element_type=F32,
                )
                total = term if total is None else total + term
            give(k, 1, rr, total)

    def collect(k):
        for src in range(GROUPS * R):

            @pl.when(src != me)
            def _():
                remote(
                    pbuf.at[k, src], pbuf.at[k, src], y_s.at[0, 0], y_r.at[k, src], {"row": r}
                ).wait_recv()

        total = pbuf[k, 0]
        for src in range(1, GROUPS * R):
            total = total + pbuf[k, src]
        scale = scales[:, pl.ds(pl.multiple_of(r * piece, piece), piece)]
        state = jnp.where(g == 0, total, scale * total)
        ubuf[...] = state
        tsend[k] = state.astype(BF)
        for kind in range(GROUPS):
            for rr in range(R):

                @pl.when((g != kind) | (r != rr))
                def _():
                    y_copy(k, kind, rr).wait_send()

    acc[...] = outer_part(0, 0, everything)
    for xx in range(1, X - 1):
        acc[...] += outer_part(0, xx, everything)
    send_rows(0, X - 1)
    inner_rows(0)
    collect(0)

    def t_copy(k, plane, dz):
        return remote(
            tsend.at[k - 1],
            tbuf.at[k, g, z],
            t_s.at[plane, dz],
            t_r.at[k, g, z],
            {"grp": plane, "row": r, "col": col_of((z + dz) % Z, x)},
        )

    def t_each(k, act):
        for dz in order:
            for plane in range(GROUPS):
                wanted = (g == 1) | (plane == parity)
                if dz == 0:
                    wanted = wanted & (plane != g)

                @pl.when(wanted)
                def _():
                    act(t_copy(k, plane, dz))

    def iteration(k, carry):
        t_each(k, lambda copy: copy.start())

        @pl.when((g == 1) | (parity == 0))
        def _():
            tbuf[k, g, z] = tsend[k - 1]

        for zz in range(Z):

            @pl.when((zz != z) | (g != 1))
            def _():
                remote(
                    tbuf.at[k, 1, zz], tbuf.at[k, 1, zz], t_s.at[0, 0], t_r.at[k, 1, zz], {"row": r}
                ).wait_recv()

        for zi in range(Zh):
            zs = GROUPS * zi + g

            @pl.when((zs != z) | (g != 0))
            def _():
                remote(
                    tbuf.at[k, 0, zs], tbuf.at[k, 0, zs], t_s.at[0, 0], t_r.at[k, 0, zs], {"row": r}
                ).wait_recv()

        for zi in range(Zh):
            zs = GROUPS * zi + g
            choice = metabuf[zs, 0:1, :]
            far = tbuf[k, 1, g].astype(F32)
            for n in range(1, Zh):
                far = jnp.where(choice == n, tbuf[k, 1, GROUPS * n + g].astype(F32), far)
            mixed = bbuf[0, zs].astype(F32) + robin_weight * (far - tbuf[k, 0, zs].astype(F32))
            we[k, x, zi] = mixed.astype(BF)
        for dx in x_order:
            we_copy(k, dx).start()

        near = None
        for j in range(GROUPS):
            for zz in range(GROUPS):
                source = tbuf[k, 1, zz].astype(F32)
                for n in range(1, Zh):
                    other = tbuf[k, 1, GROUPS * n + zz].astype(F32)
                    source = jnp.where(adj[j, s] == n, other, source)
                term = jnp.dot(
                    source.astype(BF), gbuf[j * GROUPS + zz], preferred_element_type=F32
                )
                near = term if near is None else near + term
        for xx in range(X):
            nsend[k, xx] = near[:, xx * piece : (xx + 1) * piece].astype(BF)
        for dx in x_order:
            n_copy(k, dx).start()

        acc[...] = outer_part(k, x, everything)

        near = nsend[k, x].astype(F32)
        for dx in range(1, X):
            xs = (x + dx) % X
            x_wait(nbuf.at[k, xs], k, 1, dx)
            near = near + nbuf[k, xs].astype(F32)
        inner = tbuf[k, 1, zt].astype(F32)
        outer = tbuf[k, 0, zt].astype(F32)
        mixed = (
            bbuf[1, zt].astype(F32)
            + robin_weight * (outer - inner)
            + iface_weight * (near - inner)
        )
        wi[k, x] = mixed.astype(BF)
        for dx in x_order:
            wi_copy(k, dx).start()

        x_near = x_order[::-1]
        for dx in x_near[:-1]:
            xs = (x + dx) % X
            x_wait(we.at[k, xs], k, 0, dx)
            acc[...] += outer_part(k, xs, everything)
        if X > 1:
            xs = (x + x_near[-1]) % X
            x_wait(we.at[k, xs], k, 0, x_near[-1])
        send_rows(k, xs if X > 1 else x)
        for dx in x_near:
            x_wait(wi.at[k, (x + dx) % X], k, 2, dx)
        inner_rows(k)
        collect(k)
        for dx in x_order:
            we_copy(k, dx).wait_send()
            n_copy(k, dx).wait_send()
            wi_copy(k, dx).wait_send()
        t_each(k, lambda copy: copy.wait_send())
        return carry

    lax.fori_loop(1, ITERS, iteration, 0)
    out[0] = ubuf[...]


def body(
    excitation,
    panel_points,
    panel_areas,
    panel_map,
    interior_inverse,
    row_scales,
    iface_slot,
    iface_offset,
    adjacency,
):
    strips = lax.axis_size("col")
    R = lax.axis_size("row")
    _, rhs, piece = excitation.shape
    block = strips * piece
    sub_width = interior_inverse.shape[3]
    X = sub_width // (GROUPS * piece)
    Z = strips // X
    Zh = Z // GROUPS
    RP = R * piece
    P_ = X * Zh
    vm = pltpu.VMEM
    dma = pltpu.SemaphoreType.DMA
    in_vmem = pl.BlockSpec(memory_space=pltpu.VMEM)
    return pl.pallas_call(
        functools.partial(kernel, (Z, X, R, piece, block)),
        out_shape=jax.ShapeDtypeStruct((1, rhs, piece), F32),
        in_specs=[in_vmem] * 6
        + [pl.BlockSpec(memory_space=pltpu.SMEM), pl.BlockSpec(memory_space=pl.ANY), in_vmem],
        out_specs=in_vmem,
        scratch_shapes=[
            vm((8, RP), F32),
            vm((8, piece), F32),
            vm((P_ * piece, 8), F32),
            vm((X, Zh, piece, RP), BF),
            vm((RP, X * piece), BF),
            vm((GROUPS * GROUPS, piece, X * piece), BF),
            vm((8, piece), jnp.int32),
            vm((Z, 8, piece), jnp.int32),
            vm((X, 8, piece), jnp.int32),
            vm((GROUPS, Z, rhs, piece), BF),
            vm((ITERS, rhs, piece), BF),
            vm((ITERS, GROUPS, Z, rhs, piece), BF),
            vm((ITERS, X, Zh, rhs, piece), BF),
            vm((ITERS, X, rhs, piece), BF),
            vm((ITERS, X, rhs, piece), BF),
            vm((ITERS, X, rhs, piece), BF),
            vm((rhs, RP), F32),
            vm((ITERS, GROUPS, R, rhs, piece), F32),
            vm((ITERS, GROUPS * R, rhs, piece), F32),
            vm((rhs, piece), F32),
            dma(()),
            dma((Z,)),
            dma((GROUPS, Z)),
            dma((Z,)),
            dma((Z,)),
            dma((GROUPS, Z)),
            dma((ITERS, GROUPS, Z)),
            dma((3, X)),
            dma((ITERS, 3, X)),
            dma((GROUPS, R)),
            dma((ITERS, GROUPS * R)),
        ],
        compiler_params=pltpu.CompilerParams(
            collective_id=0, has_side_effects=True, vmem_limit_bytes=60 * 1024 * 1024
        ),
    )(
        excitation,
        panel_points,
        panel_areas.reshape(1, -1),
        panel_map.reshape(1, -1),
        iface_slot.reshape(1, -1),
        iface_offset.reshape(1, -1),
        adjacency.T,
        interior_inverse[0, :, 0, :],
        row_scales,
    )


def solution(mesh):
    placed = (
        P("grp", None, ("row", "col")),
        P(),
        P(),
        P(("row", "col")),
        P("col", None, "row", None),
        P("col", None),
        P(("row", "col")),
        P(("row", "col")),
        P(),
    )
    return jax.shard_map(
        body, mesh=mesh, in_specs=placed, out_specs=P("grp", None, ("row", "col")), check_vma=False
    )
```

time: 499 us -> 99.6 us (0.20)
  other arithmetic: 152 us -> 0 us
  local copies, waits for them, and re-layouts: 127 us -> 1.32 us
  blocking collectives: 125 us -> 0 us
  Pallas kernels: 0 us -> 97.2 us
  matrix products: 41 us -> 0 us
  starting transfers between devices: 24.9 us -> 0 us
  waiting for transfers between devices: 21.8 us -> 0 us
  loops' own time: 5.61 us -> 0 us
    dynamic_update_slice x8 -> x0, other arithmetic: 147 us -> none  [make_tiles(): made = lax.map(one_tile, jnp.arange(count, dtype=jnp.int32))]
    all_to_all x9 -> x0, blocking collectives: 125 us -> none  [the longest x6 89.9 us: from_everyone(): lax.all_to_all(jnp.broadcast_to(shard[None], (peers, *shard.shape)), axis...]
    pallas_call x0 -> x1, Pallas kernels: none -> 97.2 us  [body(): pl.pallas_call(functools.partial(kernel, (Z, X, R, piece, block)), out_sh...]
    gather x24 -> x0, local copies, waits for them, and re-layouts: 75.9 us -> none  [the longest x8 68.6 us: kernel_block(): row_points = jnp.take(panel_points, row_ids, axis=1)]
    dot_general x4 -> x0, matrix products: 41 us -> none  [exterior_range(): lax.dot_general(columns, kept_tiles, (((1, 2), (0, 2)), ((), ())), prefer...]
    slice x8 -> x0, local copies, waits for them, and re-layouts: 23.8 us -> none  [kernel_block(): square = (row_points[0][:, None] - col_points[0][None, :]) ** 2]
    all_to_all x3 -> x0, starting transfers between devices: 22.4 us -> none  [the longest x2 15.9 us: from_everyone(): lax.all_to_all(jnp.broadcast_to(shard[None], (peers, *shard.shape)), axis...]
    all_to_all x3 -> x0, waiting for transfers between devices: 14.3 us -> none  [the longest x2 9.58 us: from_everyone(): lax.all_to_all(jnp.broadcast_to(shard[None], (peers, *shard.shape)), axis...]
  transfers between devices with their start and end apart: 7 -> 0, of which waited for: 5 -> 0; matrix products, arithmetic and copies ran while one was open for 53% -> 0% of each run, Pallas kernels for 0% -> 0%
where the time goes in v1:
time: 99.6 us; the launch traced here: 98.5 us
  Pallas kernels  97.2 us (98%)
  local copies, waits for them, and re-layouts  1.32 us (1%)
    pallas_call x1, Pallas kernels, body(): pl.pallas_call(functools.partial(kernel, (Z, X, R, piece, block)), out_sh...  97.2 us

profile of v1, /device:TPU:1, one launch (start us, length us, event | category | flops | bytes accessed | tf_op | source)
XLA Modules:
  0.0 98.5 jit_solution(13563952089429205632)
XLA Ops:
  0.0 97.2 %shard_map.91 = f32[1,16,256]{2,1,0:T(8,128)} custom-call(bf16[1,16,256]{2,1,0:T(8,128)(2,1)} %exc.1, f32[3,32768]{1,0:T(4,128)} %pts.1, f32[1,32768]{1,0:T(1,128)} %bitcast.7, s32[1,256]{1,0:T(1,128)} %bitcast.8, s32[1,256]{1,0:T(1,128)} %bitcast.9, s32[1,256]{1,0:T(1,128)} %bitcast.10, s32[2,4]{1,0:T(2,128)} %bitcast.11, bf16[1024,2048]{1,0:T(8,128)(2,1)} %bitcast.6, ...), custom_call_target="tpu_custom_call" | custom-call | tf_op jit(solution)/shard_map/pallas_call | solution.py:532
  97.2 1.3 %copy.11 = f32[1,16,256]{2,1,0:T(8,128)} copy(f32[1,16,256]{2,1,0:T(8,128)} %shard_map.91) | data formatting | bytes 32768

commit v2 on v1

--- a/solution.py
+++ b/solution.py
@@ -47,6 +47,7 @@
     ipt,
     stage,
     kpt,
+    kline,
     kbuf,
     abuf,
     gbuf,
@@ -134,42 +135,61 @@
 
     for rr in range(R):
         start = pl.multiple_of(rr * block + c * piece, piece)
-        ipt[0:3, rr * piece : (rr + 1) * piece] = pts[:, pl.ds(start, piece)] * TURNS
-    stage[...] = jnp.zeros_like(stage)
-
-    def stage_points(p, carry):
+        own = pts[:, pl.ds(start, piece)] * TURNS
+        for axis in range(3):
+            ipt[axis, :, rr * piece : (rr + 1) * piece] = jnp.broadcast_to(
+                own[axis : axis + 1, :], (KB, piece)
+            )
+    for p in range(X * Zh):
         xx, zi = p // Zh, p % Zh
         start = pl.multiple_of(r * block + col_of(GROUPS * zi + g, xx) * piece, piece)
-        stage[0:3, :] = pts[:, pl.ds(start, piece)] * TURNS
-        stage[3:4, :] = areas[:, pl.ds(start, piece)] * TURNS
-        kpt[pl.ds(pl.multiple_of(p * piece, piece), piece), :] = jnp.transpose(stage[...])
-        return carry
-
-    lax.fori_loop(0, X * Zh, stage_points, 0)
+        lanes = slice(p * piece, (p + 1) * piece)
+        stage[0:3, lanes] = pts[:, pl.ds(start, piece)] * TURNS
+        area = areas[:, pl.ds(start, piece)] * TURNS
+        stage[3:4, lanes] = area
+        root = jnp.sqrt(area)
+        for n, term in enumerate(COS_TERMS):
+            stage[4 + n : 5 + n, lanes] = root * term
+        stage[9:16, lanes] = jnp.zeros((7, piece), F32)
+    kpt[...] = jnp.transpose(stage[...])
 
     per_piece = piece // KB
+    last_block = X * Zh * per_piece - 1
+    LANES = 128
+    PAIR = min(RP, 2 * LANES)
+
+    def spread(t, to):
+        kc = kpt[pl.ds(pl.multiple_of(t * KB, KB), KB), :]
+        for n in range(9):
+            kline[to, n] = jnp.broadcast_to(kc[:, n : n + 1], (KB, LANES))
+
+    spread(0, 0)
 
     def make_rows(t, carry):
         p = t // per_piece
         row = pl.multiple_of((t % per_piece) * KB, KB)
-        kc = kpt[pl.ds(pl.multiple_of(t * KB, KB), KB), :]
-        ix, iy, iz = ipt[0:1, :], ipt[1:2, :], ipt[2:3, :]
-        dx = ix - kc[:, 0:1]
-        dy = iy - kc[:, 1:2]
-        dz = iz - kc[:, 2:3]
-        square = dx * dx + dy * dy
-        square = jnp.maximum(square + dz * dz, 1e-30)
-        turns = square * lax.rsqrt(square)
-        part = turns - jnp.round(turns)
-        v = part * part
-        h = COS_TERMS[4] * v + COS_TERMS[3]
-        h = h * v + COS_TERMS[2]
-        h = h * v + COS_TERMS[1]
-        h = h * v + COS_TERMS[0]
-        area = kc[:, 3:4]
-        top = area * (h * h) - area
-        value = top / (turns + soften * TURNS)
-        kbuf[p // Zh, p % Zh, pl.ds(row, KB), :] = value.astype(BF)
+        now = t % 2
+        for m in range(RP // PAIR):
+            halves = []
+            for half in range(PAIR // LANES):
+                first = m * PAIR + half * LANES
+                lanes = slice(first, first + LANES)
+                dx = ipt[0, :, lanes] - kline[now, 0]
+                dy = ipt[1, :, lanes] - kline[now, 1]
+                dz = ipt[2, :, lanes] - kline[now, 2]
+                square = dx * dx + dy * dy + dz * dz
+                turns = 1.0 / lax.rsqrt(square)
+                part = turns - jnp.round(turns)
+                v = part * part
+                h = kline[now, 8] * v + kline[now, 7]
+                h = h * v + kline[now, 6]
+                h = h * v + kline[now, 5]
+                h = h * v + kline[now, 4]
+                top = h * h - kline[now, 3]
+                halves.append(top / (turns + soften * TURNS))
+            value = jnp.concatenate(halves, axis=1).astype(BF)
+            kbuf[p // Zh, p % Zh, pl.ds(row, KB), m * PAIR : (m + 1) * PAIR] = value
+        spread(jnp.minimum(t + 1, last_block), 1 - now)
         return carry
 
     quarter = X * Zh * per_piece // 4
@@ -435,17 +455,6 @@
                 remote(
                     tbuf.at[k, 0, zs], tbuf.at[k, 0, zs], t_s.at[0, 0], t_r.at[k, 0, zs], {"row": r}
                 ).wait_recv()
-
-        for zi in range(Zh):
-            zs = GROUPS * zi + g
-            choice = metabuf[zs, 0:1, :]
-            far = tbuf[k, 1, g].astype(F32)
-            for n in range(1, Zh):
-                far = jnp.where(choice == n, tbuf[k, 1, GROUPS * n + g].astype(F32), far)
-            mixed = bbuf[0, zs].astype(F32) + robin_weight * (far - tbuf[k, 0, zs].astype(F32))
-            we[k, x, zi] = mixed.astype(BF)
-        for dx in x_order:
-            we_copy(k, dx).start()
 
         near = None
         for j in range(GROUPS):
@@ -462,6 +471,17 @@
             nsend[k, xx] = near[:, xx * piece : (xx + 1) * piece].astype(BF)
         for dx in x_order:
             n_copy(k, dx).start()
+
+        for zi in range(Zh):
+            zs = GROUPS * zi + g
+            choice = metabuf[zs, 0:1, :]
+            far = tbuf[k, 1, g].astype(F32)
+            for n in range(1, Zh):
+                far = jnp.where(choice == n, tbuf[k, 1, GROUPS * n + g].astype(F32), far)
+            mixed = bbuf[0, zs].astype(F32) + robin_weight * (far - tbuf[k, 0, zs].astype(F32))
+            we[k, x, zi] = mixed.astype(BF)
+        for dx in x_order:
+            we_copy(k, dx).start()
 
         acc[...] = outer_part(k, x, everything)
 
@@ -536,9 +556,10 @@
         + [pl.BlockSpec(memory_space=pltpu.SMEM), pl.BlockSpec(memory_space=pl.ANY), in_vmem],
         out_specs=in_vmem,
         scratch_shapes=[
-            vm((8, RP), F32),
-            vm((8, piece), F32),
-            vm((P_ * piece, 8), F32),
+            vm((3, KB, RP), F32),
+            vm((16, P_ * piece), F32),
+            vm((P_ * piece, 16), F32),
+            vm((2, 9, KB, 128), F32),
             vm((X, Zh, piece, RP), BF),
             vm((RP, X * piece), BF),
             vm((GROUPS * GROUPS, piece, X * piece), BF),

time: 99.6 us -> 90.2 us (0.906)
  Pallas kernels: 97.2 us -> 88.6 us
    pallas_call x1, Pallas kernels: 97.2 us -> 88.6 us  [body(): pl.pallas_call(functools.partial(kernel, (Z, X, R, piece, block)), out_sh...]
where the time goes in v2:
time: 90.2 us; the launch traced here: 89.9 us
  Pallas kernels  88.6 us (98%)
  local copies, waits for them, and re-layouts  1.32 us (1%)
    pallas_call x1, Pallas kernels, body(): pl.pallas_call(functools.partial(kernel, (Z, X, R, piece, block)), out_sh...  88.6 us

profile of v2, /device:TPU:1, one launch (start us, length us, event | category | flops | bytes accessed | tf_op | source)
XLA Modules:
  0.0 89.9 jit_solution(9007774852642818577)
XLA Ops:
  0.0 88.6 %shard_map.91 = f32[1,16,256]{2,1,0:T(8,128)} custom-call(bf16[1,16,256]{2,1,0:T(8,128)(2,1)} %exc.1, f32[3,32768]{1,0:T(4,128)} %pts.1, f32[1,32768]{1,0:T(1,128)} %bitcast.7, s32[1,256]{1,0:T(1,128)} %bitcast.8, s32[1,256]{1,0:T(1,128)} %bitcast.9, s32[1,256]{1,0:T(1,128)} %bitcast.10, s32[2,4]{1,0:T(2,128)} %bitcast.11, bf16[1024,2048]{1,0:T(8,128)(2,1)} %bitcast.6, ...), custom_call_target="tpu_custom_call" | custom-call | tf_op jit(solution)/shard_map/pallas_call | solution.py:552
  88.6 1.3 %copy.11 = f32[1,16,256]{2,1,0:T(8,128)} copy(f32[1,16,256]{2,1,0:T(8,128)} %shard_map.91) | data formatting | bytes 32768

commit v3 on v2

--- a/solution.py
+++ b/solution.py
@@ -192,12 +192,13 @@
         spread(jnp.minimum(t + 1, last_block), 1 - now)
         return carry
 
-    quarter = X * Zh * per_piece // 4
-
-    def make_quarter(q):
-        lax.fori_loop(q * quarter, (q + 1) * quarter, make_rows, 0)
-
-    make_quarter(0)
+    trips = X * Zh * per_piece
+    cuts = (0, trips * 7 // 16, trips * 12 // 16, trips)
+
+    def make_part(q):
+        lax.fori_loop(cuts[q], cuts[q + 1], make_rows, 0)
+
+    make_part(0)
     pl.semaphore_wait(barrier, n_partners)
 
     metasend[...] = jnp.zeros_like(metasend)
@@ -242,7 +243,7 @@
                 bbuf[g, z] = exc[0]
                 metabuf[z] = metasend[...]
 
-    make_quarter(1)
+    make_part(1)
 
     for zi in range(Zh):
         zs = GROUPS * zi + g
@@ -289,11 +290,7 @@
         we_copy(0, dx).start()
         xm_copy(dx).start()
         wi_copy(0, dx).start()
-    make_quarter(2)
-
-    for dx in range(1, X):
-        xs = (x + dx) % X
-        x_wait(xmeta.at[xs], 0, 1, dx)
+    make_part(2)
 
     def make_gather(t, carry):
         xx, q = t // (GROUPS * GROUPS), t % (GROUPS * GROUPS)
@@ -306,12 +303,11 @@
         gbuf[q, :, pl.ds(pl.multiple_of(xx * piece, piece), piece)] = hit
         return carry
 
-    lax.fori_loop(0, X * GROUPS * GROUPS, make_gather, 0)
-    make_quarter(3)
     inverse_copy.wait()
     for dx in range(1, X):
         x_wait(we.at[0, (x + dx) % X], 0, 0, dx)
         x_wait(wi.at[0, (x + dx) % X], 0, 2, dx)
+        x_wait(xmeta.at[(x + dx) % X], 0, 1, dx)
         we_copy(0, dx).wait_send()
         xm_copy(dx).wait_send()
         wi_copy(0, dx).wait_send()
@@ -328,26 +324,42 @@
             def _():
                 b_copy(0).wait_send()
 
-    def y_copy(k, kind, rr):
+    def is_last(k):
+        return jnp.int32(k) == ITERS - 1
+
+    def y_plane(k, way):
+        return jnp.where(is_last(k), 0, parity) if way == 0 else 2 - way
+
+    def y_copy(k, way, rr):
+        kind = min(way, 1)
         return remote(
             psend.at[k, kind, rr],
-            pbuf.at[k, me],
-            y_s.at[kind, rr],
-            y_r.at[k, me],
-            {"grp": kind, "row": rr, "col": c},
-        )
+            pbuf.at[k, kind, me],
+            y_s.at[way, rr],
+            y_r.at[k, kind, me],
+            {"grp": y_plane(k, way), "row": rr, "col": c},
+        )
+
+    def y_other(k, way, rr):
+        other = (g != y_plane(k, way)) | (r != rr)
+        return other & jnp.logical_not(is_last(k)) if way == 2 else other
 
     def give(k, kind, rr, value):
         psend[k, kind, rr] = value
-        own = (g == kind) & (r == rr)
-
-        @pl.when(jnp.logical_not(own))
-        def _():
-            y_copy(k, kind, rr).start()
-
-        @pl.when(own)
-        def _():
-            pbuf[k, me] = value
+        for way in ((0,), (1, 2))[kind]:
+
+            @pl.when(y_other(k, way, rr))
+            def _():
+                y_copy(k, way, rr).start()
+
+    def t_copy(k, kind, dz):
+        return remote(
+            tsend.at[k, kind],
+            tbuf.at[k + 1, kind, z],
+            t_s.at[kind, dz],
+            t_r.at[k + 1, kind, z],
+            {"grp": g, "row": r, "col": col_of((z + dz) % Z, x)},
+        )
 
     def outer_part(k, xs, columns):
         total = None
@@ -383,65 +395,74 @@
             give(k, 1, rr, total)
 
     def collect(k):
-        for src in range(GROUPS * R):
-
-            @pl.when(src != me)
-            def _():
-                remote(
-                    pbuf.at[k, src], pbuf.at[k, src], y_s.at[0, 0], y_r.at[k, src], {"row": r}
-                ).wait_recv()
-
-        total = pbuf[k, 0]
-        for src in range(1, GROUPS * R):
-            total = total + pbuf[k, src]
-        scale = scales[:, pl.ds(pl.multiple_of(r * piece, piece), piece)]
-        state = jnp.where(g == 0, total, scale * total)
-        ubuf[...] = state
-        tsend[k] = state.astype(BF)
         for kind in range(GROUPS):
+            takes = (
+                jnp.where(is_last(k), 0, parity) == g
+                if kind == 0
+                else jnp.logical_not(is_last(k)) | (g == 1)
+            )
+            for src in range(GROUPS * R):
+
+                @pl.when(takes & (src != me))
+                def _():
+                    remote(
+                        pbuf.at[k, kind, src],
+                        pbuf.at[k, kind, src],
+                        y_s.at[0, 0],
+                        y_r.at[k, kind, src],
+                        {"row": r},
+                    ).wait_recv()
+
+            @pl.when(takes)
+            def _():
+                pbuf[k, kind, me] = psend[k, kind, r]
+                total = pbuf[k, kind, 0]
+                for src in range(1, GROUPS * R):
+                    total = total + pbuf[k, kind, src]
+                if kind == 1:
+                    total = total * scales[:, pl.ds(pl.multiple_of(r * piece, piece), piece)]
+
+                @pl.when(is_last(k))
+                def _():
+                    ubuf[...] = total
+
+                @pl.when(jnp.logical_not(is_last(k)))
+                def _():
+                    trace = total.astype(BF)
+                    tsend[k, kind] = trace
+                    for dz in order:
+                        if dz:
+                            t_copy(k, kind, dz).start()
+                    tbuf[k + 1, kind, z] = trace
+
+        for way in range(3):
             for rr in range(R):
 
-                @pl.when((g != kind) | (r != rr))
+                @pl.when(y_other(k, way, rr))
                 def _():
-                    y_copy(k, kind, rr).wait_send()
+                    y_copy(k, way, rr).wait_send()
+
+    def t_sent(k):
+        for kind in range(GROUPS):
+
+            @pl.when((kind == 1) | (parity == g))
+            def _():
+                for dz in order:
+                    if dz:
+                        t_copy(k, kind, dz).wait_send()
 
     acc[...] = outer_part(0, 0, everything)
     for xx in range(1, X - 1):
         acc[...] += outer_part(0, xx, everything)
     send_rows(0, X - 1)
     inner_rows(0)
+    lax.fori_loop(0, X * GROUPS * GROUPS, make_gather, 0)
     collect(0)
 
-    def t_copy(k, plane, dz):
-        return remote(
-            tsend.at[k - 1],
-            tbuf.at[k, g, z],
-            t_s.at[plane, dz],
-            t_r.at[k, g, z],
-            {"grp": plane, "row": r, "col": col_of((z + dz) % Z, x)},
-        )
-
-    def t_each(k, act):
-        for dz in order:
-            for plane in range(GROUPS):
-                wanted = (g == 1) | (plane == parity)
-                if dz == 0:
-                    wanted = wanted & (plane != g)
-
-                @pl.when(wanted)
-                def _():
-                    act(t_copy(k, plane, dz))
-
     def iteration(k, carry):
-        t_each(k, lambda copy: copy.start())
-
-        @pl.when((g == 1) | (parity == 0))
-        def _():
-            tbuf[k, g, z] = tsend[k - 1]
-
         for zz in range(Z):
 
-            @pl.when((zz != z) | (g != 1))
+            @pl.when(zz != z)
             def _():
                 remote(
                     tbuf.at[k, 1, zz], tbuf.at[k, 1, zz], t_s.at[0, 0], t_r.at[k, 1, zz], {"row": r}
@@ -450,7 +471,7 @@
         for zi in range(Zh):
             zs = GROUPS * zi + g
 
-            @pl.when((zs != z) | (g != 0))
+            @pl.when(zs != z)
             def _():
                 remote(
                     tbuf.at[k, 0, zs], tbuf.at[k, 0, zs], t_s.at[0, 0], t_r.at[k, 0, zs], {"row": r}
@@ -513,12 +534,12 @@
         for dx in x_near:
             x_wait(wi.at[k, (x + dx) % X], k, 2, dx)
         inner_rows(k)
+        t_sent(k - 1)
         collect(k)
         for dx in x_order:
             we_copy(k, dx).wait_send()
             n_copy(k, dx).wait_send()
             wi_copy(k, dx).wait_send()
-        t_each(k, lambda copy: copy.wait_send())
         return carry
 
     lax.fori_loop(1, ITERS, iteration, 0)
@@ -567,7 +588,7 @@
             vm((Z, 8, piece), jnp.int32),
             vm((X, 8, piece), jnp.int32),
             vm((GROUPS, Z, rhs, piece), BF),
-            vm((ITERS, rhs, piece), BF),
+            vm((ITERS, GROUPS, rhs, piece), BF),
             vm((ITERS, GROUPS, Z, rhs, piece), BF),
             vm((ITERS, X, Zh, rhs, piece), BF),
             vm((ITERS, X, rhs, piece), BF),
@@ -575,7 +596,7 @@
             vm((ITERS, X, rhs, piece), BF),
             vm((rhs, RP), F32),
             vm((ITERS, GROUPS, R, rhs, piece), F32),
-            vm((ITERS, GROUPS * R, rhs, piece), F32),
+            vm((ITERS, GROUPS, GROUPS * R, rhs, piece), F32),
             vm((rhs, piece), F32),
             dma(()),
             dma((Z,)),
@@ -586,8 +607,8 @@
             dma((ITERS, GROUPS, Z)),
             dma((3, X)),
             dma((ITERS, 3, X)),
-            dma((GROUPS, R)),
-            dma((ITERS, GROUPS * R)),
+            dma((3, R)),
+            dma((ITERS, GROUPS, GROUPS * R)),
         ],
         compiler_params=pltpu.CompilerParams(
             collective_id=0, has_side_effects=True, vmem_limit_bytes=60 * 1024 * 1024

time: 90.2 us -> 87.9 us (0.975)
  Pallas kernels: 88.6 us -> 85.8 us
    pallas_call x1, Pallas kernels: 88.6 us -> 85.8 us  [body(): pl.pallas_call(functools.partial(kernel, (Z, X, R, piece, block)), out_sh...]
where the time goes in v3:
time: 87.9 us; the launch traced here: 87.1 us
  Pallas kernels  85.8 us (98%)
  local copies, waits for them, and re-layouts  1.32 us (2%)
    pallas_call x1, Pallas kernels, body(): pl.pallas_call(functools.partial(kernel, (Z, X, R, piece, block)), out_sh...  85.8 us

profile of v3, /device:TPU:1, one launch (start us, length us, event | category | flops | bytes accessed | tf_op | source)
XLA Modules:
  0.0 87.1 jit_solution(1866957797640279032)
XLA Ops:
  0.0 85.8 %shard_map.91 = f32[1,16,256]{2,1,0:T(8,128)} custom-call(bf16[1,16,256]{2,1,0:T(8,128)(2,1)} %exc.1, f32[3,32768]{1,0:T(4,128)} %pts.1, f32[1,32768]{1,0:T(1,128)} %bitcast.7, s32[1,256]{1,0:T(1,128)} %bitcast.8, s32[1,256]{1,0:T(1,128)} %bitcast.9, s32[1,256]{1,0:T(1,128)} %bitcast.10, s32[2,4]{1,0:T(2,128)} %bitcast.11, bf16[1024,2048]{1,0:T(8,128)(2,1)} %bitcast.6, ...), custom_call_target="tpu_custom_call" | custom-call | tf_op jit(solution)/shard_map/pallas_call | solution.py:573
  85.8 1.3 %copy.11 = f32[1,16,256]{2,1,0:T(8,128)} copy(f32[1,16,256]{2,1,0:T(8,128)} %shard_map.91) | data formatting | bytes 32768

commit v4 on v3

--- a/solution.py
+++ b/solution.py
@@ -62,6 +62,7 @@
     nbuf,
     wi,
     acc,
+    inner,
     psend,
     pbuf,
     ubuf,
@@ -369,30 +370,34 @@
         return total
 
     everything = slice(None)
+    cores = min(R, 2)
+    row_order = []
+    for far in reversed(range(R // cores)):
+        for side in reversed(range(cores)):
+            row_order.append(
+                ((r // cores + far) % (R // cores)) * cores + (r % cores + side) % cores
+            )
 
     def send_rows(k, xs):
-        for j in range(R):
-            rr = (r + 1 + j) % R
+        for rr in row_order:
             columns = pl.ds(pl.multiple_of(rr * piece, piece), piece)
             value = acc[:, columns] + outer_part(k, xs, columns)
             own_piece = self_term * we[k, x, z // GROUPS].astype(F32)
             value = value + jnp.where((rr == r) & (parity == g), own_piece, 0.0)
             give(k, 0, rr, value)
 
-    def inner_rows(k):
-        for j in range(R):
-            rr = (r + 1 + j) % R
+    def inner_part(k, xs, rows):
+        return lax.dot_general(
+            wi[k, xs],
+            abuf[rows, pl.ds(pl.multiple_of(xs * piece, piece), piece)],
+            (((1,), (1,)), ((), ())),
+            preferred_element_type=F32,
+        )
+
+    def inner_rows(k, xs):
+        for rr in row_order:
             rows = pl.ds(pl.multiple_of(rr * piece, piece), piece)
-            total = None
-            for xx in range(X):
-                term = lax.dot_general(
-                    wi[k, xx],
-                    abuf[rows, xx * piece : (xx + 1) * piece],
-                    (((1,), (1,)), ((), ())),
-                    preferred_element_type=F32,
-                )
-                total = term if total is None else total + term
-            give(k, 1, rr, total)
+            give(k, 1, rr, inner[:, rows] + inner_part(k, xs, rows))
 
     def collect(k):
         for kind in range(GROUPS):
@@ -455,7 +460,10 @@
     for xx in range(1, X - 1):
         acc[...] += outer_part(0, xx, everything)
     send_rows(0, X - 1)
-    inner_rows(0)
+    inner[...] = inner_part(0, 0, everything)
+    for xx in range(1, X - 1):
+        inner[...] += inner_part(0, xx, everything)
+    inner_rows(0, X - 1)
     lax.fori_loop(0, X * GROUPS * GROUPS, make_gather, 0)
     collect(0)
 
@@ -477,21 +485,24 @@
                     tbuf.at[k, 0, zs], tbuf.at[k, 0, zs], t_s.at[0, 0], t_r.at[k, 0, zs], {"row": r}
                 ).wait_recv()
 
-        near = None
+        sources = []
         for j in range(GROUPS):
             for zz in range(GROUPS):
                 source = tbuf[k, 1, zz].astype(F32)
                 for n in range(1, Zh):
                     other = tbuf[k, 1, GROUPS * n + zz].astype(F32)
                     source = jnp.where(adj[j, s] == n, other, source)
-                term = jnp.dot(
-                    source.astype(BF), gbuf[j * GROUPS + zz], preferred_element_type=F32
-                )
+                sources.append(source.astype(BF))
+        for dx in x_order + [0]:
+            xx = (x + dx) % X
+            columns = pl.ds(pl.multiple_of(xx * piece, piece), piece)
+            near = None
+            for q, source in enumerate(sources):
+                term = jnp.dot(source, gbuf[q, :, columns], preferred_element_type=F32)
                 near = term if near is None else near + term
-        for xx in range(X):
-            nsend[k, xx] = near[:, xx * piece : (xx + 1) * piece].astype(BF)
-        for dx in x_order:
-            n_copy(k, dx).start()
+            nsend[k, xx] = near.astype(BF)
+            if dx:
+                n_copy(k, dx).start()
 
         for zi in range(Zh):
             zs = GROUPS * zi + g
@@ -511,12 +522,12 @@
             xs = (x + dx) % X
             x_wait(nbuf.at[k, xs], k, 1, dx)
             near = near + nbuf[k, xs].astype(F32)
-        inner = tbuf[k, 1, zt].astype(F32)
-        outer = tbuf[k, 0, zt].astype(F32)
+        own_inner = tbuf[k, 1, zt].astype(F32)
+        own_outer = tbuf[k, 0, zt].astype(F32)
         mixed = (
             bbuf[1, zt].astype(F32)
-            + robin_weight * (outer - inner)
-            + iface_weight * (near - inner)
+            + robin_weight * (own_outer - own_inner)
+            + iface_weight * (near - own_inner)
         )
         wi[k, x] = mixed.astype(BF)
         for dx in x_order:
@@ -527,13 +538,17 @@
             xs = (x + dx) % X
             x_wait(we.at[k, xs], k, 0, dx)
             acc[...] += outer_part(k, xs, everything)
-        if X > 1:
-            xs = (x + x_near[-1]) % X
-            x_wait(we.at[k, xs], k, 0, x_near[-1])
-        send_rows(k, xs if X > 1 else x)
-        for dx in x_near:
-            x_wait(wi.at[k, (x + dx) % X], k, 2, dx)
-        inner_rows(k)
+        xs = (x + x_near[-1]) % X
+        x_wait(we.at[k, xs], k, 0, x_near[-1])
+        send_rows(k, xs)
+        inner[...] = inner_part(k, x, everything)
+        for dx in x_near[:-1]:
+            xs = (x + dx) % X
+            x_wait(wi.at[k, xs], k, 2, dx)
+            inner[...] += inner_part(k, xs, everything)
+        xs = (x + x_near[-1]) % X
+        x_wait(wi.at[k, xs], k, 2, x_near[-1])
+        inner_rows(k, xs)
         t_sent(k - 1)
         collect(k)
         for dx in x_order:
@@ -595,6 +610,7 @@
             vm((ITERS, X, rhs, piece), BF),
             vm((ITERS, X, rhs, piece), BF),
             vm((rhs, RP), F32),
+            vm((rhs, RP), F32),
             vm((ITERS, GROUPS, R, rhs, piece), F32),
             vm((ITERS, GROUPS, GROUPS * R, rhs, piece), F32),
             vm((rhs, piece), F32),

time: 87.9 us -> 86.4 us (0.983)
  Pallas kernels: 85.8 us -> 84.4 us
    pallas_call x1, Pallas kernels: 85.8 us -> 84.4 us  [body(): pl.pallas_call(functools.partial(kernel, (Z, X, R, piece, block)), out_sh...]
where the time goes in v4:
time: 86.4 us; the launch traced here: 85.8 us
  Pallas kernels  84.4 us (98%)
  local copies, waits for them, and re-layouts  1.32 us (2%)
    pallas_call x1, Pallas kernels, body(): pl.pallas_call(functools.partial(kernel, (Z, X, R, piece, block)), out_sh...  84.4 us

profile of v4, /device:TPU:1, one launch (start us, length us, event | category | flops | bytes accessed | tf_op | source)
XLA Modules:
  0.0 85.8 jit_solution(11865922248122196486)
XLA Ops:
  0.0 84.4 %shard_map.91 = f32[1,16,256]{2,1,0:T(8,128)} custom-call(bf16[1,16,256]{2,1,0:T(8,128)(2,1)} %exc.1, f32[3,32768]{1,0:T(4,128)} %pts.1, f32[1,32768]{1,0:T(1,128)} %bitcast.7, s32[1,256]{1,0:T(1,128)} %bitcast.8, s32[1,256]{1,0:T(1,128)} %bitcast.9, s32[1,256]{1,0:T(1,128)} %bitcast.10, s32[2,4]{1,0:T(2,128)} %bitcast.11, bf16[1024,2048]{1,0:T(8,128)(2,1)} %bitcast.6, ...), custom_call_target="tpu_custom_call" | custom-call | tf_op jit(solution)/shard_map/pallas_call | solution.py:588
  84.4 1.3 %copy.11 = f32[1,16,256]{2,1,0:T(8,128)} copy(f32[1,16,256]{2,1,0:T(8,128)} %shard_map.91) | data formatting | bytes 32768

commit v5 on v4

--- a/solution.py
+++ b/solution.py
@@ -61,8 +61,8 @@
     nsend,
     nbuf,
     wi,
+    xtrace,
     acc,
-    inner,
     psend,
     pbuf,
     ubuf,
@@ -269,12 +269,19 @@
         return remote(we.at[k, x], we.at[k, x], x_s.at[0, dx], x_r.at[k, 0, x], x_dev(dx))
 
     def n_copy(k, dx):
-        return remote(
-            nsend.at[k, (x + dx) % X], nbuf.at[k, x], x_s.at[1, dx], x_r.at[k, 1, x], x_dev(dx)
-        )
+        return remote(nsend.at[k], nbuf.at[k, x], x_s.at[1, dx], x_r.at[k, 1, x], x_dev(dx))
 
     def wi_copy(k, dx):
         return remote(wi.at[k, x], wi.at[k, x], x_s.at[2, dx], x_r.at[k, 2, x], x_dev(dx))
+
+    def base_copy(k, kind, dx):
+        return remote(
+            tbuf.at[k, kind, zt],
+            xtrace.at[k, kind, x],
+            x_s.at[2 + kind, dx],
+            x_r.at[k, 2 + kind, x],
+            x_dev(dx),
+        )
 
     def xm_copy(dx):
         return remote(metabuf.at[zt], xmeta.at[x], x_s.at[1, dx], x_r.at[0, 1, x], x_dev(dx))
@@ -389,15 +396,19 @@
     def inner_part(k, xs, rows):
         return lax.dot_general(
             wi[k, xs],
-            abuf[rows, pl.ds(pl.multiple_of(xs * piece, piece), piece)],
+            abuf[rows, xs * piece : (xs + 1) * piece],
             (((1,), (1,)), ((), ())),
             preferred_element_type=F32,
         )
 
-    def inner_rows(k, xs):
+    def inner_rows(k, pieces):
         for rr in row_order:
             rows = pl.ds(pl.multiple_of(rr * piece, piece), piece)
-            give(k, 1, rr, inner[:, rows] + inner_part(k, xs, rows))
+            total = None
+            for xs in pieces:
+                term = inner_part(k, xs, rows)
+                total = term if total is None else total + term
+            give(k, 1, rr, total)
 
     def collect(k):
         for kind in range(GROUPS):
@@ -460,10 +471,7 @@
     for xx in range(1, X - 1):
         acc[...] += outer_part(0, xx, everything)
     send_rows(0, X - 1)
-    inner[...] = inner_part(0, 0, everything)
-    for xx in range(1, X - 1):
-        inner[...] += inner_part(0, xx, everything)
-    inner_rows(0, X - 1)
+    inner_rows(0, range(X))
     lax.fori_loop(0, X * GROUPS * GROUPS, make_gather, 0)
     collect(0)
 
@@ -484,25 +492,6 @@
                 remote(
                     tbuf.at[k, 0, zs], tbuf.at[k, 0, zs], t_s.at[0, 0], t_r.at[k, 0, zs], {"row": r}
                 ).wait_recv()
-
-        sources = []
-        for j in range(GROUPS):
-            for zz in range(GROUPS):
-                source = tbuf[k, 1, zz].astype(F32)
-                for n in range(1, Zh):
-                    other = tbuf[k, 1, GROUPS * n + zz].astype(F32)
-                    source = jnp.where(adj[j, s] == n, other, source)
-                sources.append(source.astype(BF))
-        for dx in x_order + [0]:
-            xx = (x + dx) % X
-            columns = pl.ds(pl.multiple_of(xx * piece, piece), piece)
-            near = None
-            for q, source in enumerate(sources):
-                term = jnp.dot(source, gbuf[q, :, columns], preferred_element_type=F32)
-                near = term if near is None else near + term
-            nsend[k, xx] = near.astype(BF)
-            if dx:
-                n_copy(k, dx).start()
 
         for zi in range(Zh):
             zs = GROUPS * zi + g
@@ -515,23 +504,28 @@
         for dx in x_order:
             we_copy(k, dx).start()
 
+        for dx in x_order:
+            for kind in range(GROUPS):
+                base_copy(k, kind, dx).start()
+        sources = []
+        for j in range(GROUPS):
+            for zz in range(GROUPS):
+                source = tbuf[k, 1, zz].astype(F32)
+                for n in range(1, Zh):
+                    other = tbuf[k, 1, GROUPS * n + zz].astype(F32)
+                    source = jnp.where(adj[j, s] == n, other, source)
+                sources.append(source.astype(BF))
+        for xx in range(X):
+            columns = slice(xx * piece, (xx + 1) * piece)
+            near = None
+            for q, source in enumerate(sources):
+                term = jnp.dot(source, gbuf[q, :, columns], preferred_element_type=F32)
+                near = term if near is None else near + term
+            nsend[k, xx] = near.astype(BF)
+        for dx in x_order:
+            n_copy(k, dx).start()
+
         acc[...] = outer_part(k, x, everything)
-
-        near = nsend[k, x].astype(F32)
-        for dx in range(1, X):
-            xs = (x + dx) % X
-            x_wait(nbuf.at[k, xs], k, 1, dx)
-            near = near + nbuf[k, xs].astype(F32)
-        own_inner = tbuf[k, 1, zt].astype(F32)
-        own_outer = tbuf[k, 0, zt].astype(F32)
-        mixed = (
-            bbuf[1, zt].astype(F32)
-            + robin_weight * (own_outer - own_inner)
-            + iface_weight * (near - own_inner)
-        )
-        wi[k, x] = mixed.astype(BF)
-        for dx in x_order:
-            wi_copy(k, dx).start()
 
         x_near = x_order[::-1]
         for dx in x_near[:-1]:
@@ -541,20 +535,32 @@
         xs = (x + x_near[-1]) % X
         x_wait(we.at[k, xs], k, 0, x_near[-1])
         send_rows(k, xs)
-        inner[...] = inner_part(k, x, everything)
-        for dx in x_near[:-1]:
+        for dx in x_near:
             xs = (x + dx) % X
-            x_wait(wi.at[k, xs], k, 2, dx)
-            inner[...] += inner_part(k, xs, everything)
-        xs = (x + x_near[-1]) % X
-        x_wait(wi.at[k, xs], k, 2, x_near[-1])
-        inner_rows(k, xs)
+            x_wait(nbuf.at[k, xs], k, 1, dx)
+            for kind in range(GROUPS):
+                x_wait(xtrace.at[k, kind, xs], k, 2 + kind, dx)
+        for dx in range(X):
+            xs = (x + dx) % X
+            near = nsend[k, xs].astype(F32)
+            for other in range(1, X):
+                near = near + nbuf[k, (x + other) % X, xs].astype(F32)
+            own_outer = (xtrace[k, 0, xs] if dx else tbuf[k, 0, zt]).astype(F32)
+            own_inner = (xtrace[k, 1, xs] if dx else tbuf[k, 1, zt]).astype(F32)
+            mixed = (
+                wi[0, xs].astype(F32)
+                + robin_weight * (own_outer - own_inner)
+                + iface_weight * (near - own_inner)
+            )
+            wi[k, xs] = mixed.astype(BF)
+        inner_rows(k, range(X))
         t_sent(k - 1)
         collect(k)
         for dx in x_order:
             we_copy(k, dx).wait_send()
             n_copy(k, dx).wait_send()
-            wi_copy(k, dx).wait_send()
+            for kind in range(GROUPS):
+                base_copy(k, kind, dx).wait_send()
         return carry
 
     lax.fori_loop(1, ITERS, iteration, 0)
@@ -607,9 +613,9 @@
             vm((ITERS, GROUPS, Z, rhs, piece), BF),
             vm((ITERS, X, Zh, rhs, piece), BF),
             vm((ITERS, X, rhs, piece), BF),
+            vm((ITERS, X, X, rhs, piece), BF),
             vm((ITERS, X, rhs, piece), BF),
-            vm((ITERS, X, rhs, piece), BF),
-            vm((rhs, RP), F32),
+            vm((ITERS, GROUPS, X, rhs, piece), BF),
             vm((rhs, RP), F32),
             vm((ITERS, GROUPS, R, rhs, piece), F32),
             vm((ITERS, GROUPS, GROUPS * R, rhs, piece), F32),
@@ -621,8 +627,8 @@
             dma((Z,)),
             dma((GROUPS, Z)),
             dma((ITERS, GROUPS, Z)),
-            dma((3, X)),
-            dma((ITERS, 3, X)),
+            dma((4, X)),
+            dma((ITERS, 4, X)),
             dma((3, R)),
             dma((ITERS, GROUPS, GROUPS * R)),
         ],

time: 86.4 us -> 82.4 us (0.954)
  Pallas kernels: 84.4 us -> 80.9 us
    pallas_call x1, Pallas kernels: 84.4 us -> 80.9 us  [body(): pl.pallas_call(functools.partial(kernel, (Z, X, R, piece, block)), out_sh...]
where the time goes in v5:
time: 82.4 us; the launch traced here: 82.2 us
  Pallas kernels  80.9 us (98%)
  local copies, waits for them, and re-layouts  1.32 us (2%)
    pallas_call x1, Pallas kernels, body(): pl.pallas_call(functools.partial(kernel, (Z, X, R, piece, block)), out_sh...  80.9 us

profile of v5, /device:TPU:1, one launch (start us, length us, event | category | flops | bytes accessed | tf_op | source)
XLA Modules:
  0.0 82.2 jit_solution(14886273541247269394)
XLA Ops:
  0.0 80.9 %shard_map.91 = f32[1,16,256]{2,1,0:T(8,128)} custom-call(bf16[1,16,256]{2,1,0:T(8,128)(2,1)} %exc.1, f32[3,32768]{1,0:T(4,128)} %pts.1, f32[1,32768]{1,0:T(1,128)} %bitcast.7, s32[1,256]{1,0:T(1,128)} %bitcast.8, s32[1,256]{1,0:T(1,128)} %bitcast.9, s32[1,256]{1,0:T(1,128)} %bitcast.10, s32[2,4]{1,0:T(2,128)} %bitcast.11, bf16[1024,2048]{1,0:T(8,128)(2,1)} %bitcast.6, ...), custom_call_target="tpu_custom_call" | custom-call | tf_op jit(solution)/shard_map/pallas_call | solution.py:594
  80.9 1.3 %copy.11 = f32[1,16,256]{2,1,0:T(8,128)} copy(f32[1,16,256]{2,1,0:T(8,128)} %shard_map.91) | data formatting | bytes 32768

commit v6 on v5

--- a/solution.py
+++ b/solution.py
@@ -65,7 +65,6 @@
     acc,
     psend,
     pbuf,
-    ubuf,
     asem,
     b_s,
     b_r,
@@ -316,21 +315,6 @@
         x_wait(we.at[0, (x + dx) % X], 0, 0, dx)
         x_wait(wi.at[0, (x + dx) % X], 0, 2, dx)
         x_wait(xmeta.at[(x + dx) % X], 0, 1, dx)
-        we_copy(0, dx).wait_send()
-        xm_copy(dx).wait_send()
-        wi_copy(0, dx).wait_send()
-    for dz in order:
-        if dz:
-            b_copy(dz).wait_send()
-
-            @pl.when(b_plane == g)
-            def _():
-                m_copy(dz).wait_send()
-        else:
-
-            @pl.when(b_plane != g)
-            def _():
-                b_copy(0).wait_send()
 
     def is_last(k):
         return jnp.int32(k) == ITERS - 1
@@ -440,7 +424,7 @@
 
                 @pl.when(is_last(k))
                 def _():
-                    ubuf[...] = total
+                    out[0] = total
 
                 @pl.when(jnp.logical_not(is_last(k)))
                 def _():
@@ -472,18 +456,26 @@
         acc[...] += outer_part(0, xx, everything)
     send_rows(0, X - 1)
     inner_rows(0, range(X))
+    for dx in range(1, X):
+        we_copy(0, dx).wait_send()
+        xm_copy(dx).wait_send()
+        wi_copy(0, dx).wait_send()
+    for dz in order:
+        if dz:
+            b_copy(dz).wait_send()
+
+            @pl.when(b_plane == g)
+            def _():
+                m_copy(dz).wait_send()
+        else:
+
+            @pl.when(b_plane != g)
+            def _():
+                b_copy(0).wait_send()
     lax.fori_loop(0, X * GROUPS * GROUPS, make_gather, 0)
     collect(0)
 
     def iteration(k, carry):
-        for zz in range(Z):
-
-            @pl.when(zz != z)
-            def _():
-                remote(
-                    tbuf.at[k, 1, zz], tbuf.at[k, 1, zz], t_s.at[0, 0], t_r.at[k, 1, zz], {"row": r}
-                ).wait_recv()
-
         for zi in range(Zh):
             zs = GROUPS * zi + g
 
@@ -491,6 +483,15 @@
             def _():
                 remote(
                     tbuf.at[k, 0, zs], tbuf.at[k, 0, zs], t_s.at[0, 0], t_r.at[k, 0, zs], {"row": r}
+                ).wait_recv()
+
+        for zi in range(Zh):
+            zs = GROUPS * zi + g
+
+            @pl.when(zs != z)
+            def _():
+                remote(
+                    tbuf.at[k, 1, zs], tbuf.at[k, 1, zs], t_s.at[0, 0], t_r.at[k, 1, zs], {"row": r}
                 ).wait_recv()
 
         for zi in range(Zh):
@@ -504,9 +505,15 @@
         for dx in x_order:
             we_copy(k, dx).start()
 
-        for dx in x_order:
-            for kind in range(GROUPS):
-                base_copy(k, kind, dx).start()
+        for zi in range(Zh):
+            zs = GROUPS * zi + (1 - g)
+
+            @pl.when(zs != z)
+            def _():
+                remote(
+                    tbuf.at[k, 1, zs], tbuf.at[k, 1, zs], t_s.at[0, 0], t_r.at[k, 1, zs], {"row": r}
+                ).wait_recv()
+
         sources = []
         for j in range(GROUPS):
             for zz in range(GROUPS):
@@ -524,6 +531,9 @@
             nsend[k, xx] = near.astype(BF)
         for dx in x_order:
             n_copy(k, dx).start()
+        for dx in x_order:
+            for kind in range(GROUPS):
+                base_copy(k, kind, dx).start()
 
         acc[...] = outer_part(k, x, everything)
 
@@ -564,7 +574,6 @@
         return carry
 
     lax.fori_loop(1, ITERS, iteration, 0)
-    out[0] = ubuf[...]
 
 
 def body(
@@ -619,7 +628,6 @@
             vm((rhs, RP), F32),
             vm((ITERS, GROUPS, R, rhs, piece), F32),
             vm((ITERS, GROUPS, GROUPS * R, rhs, piece), F32),
-            vm((rhs, piece), F32),
             dma(()),
             dma((Z,)),
             dma((GROUPS, Z)),

time: 82.4 us -> 81.5 us (0.989)
  Pallas kernels: 80.9 us -> 79.8 us
    pallas_call x1, Pallas kernels: 80.9 us -> 79.8 us  [body(): pl.pallas_call(functools.partial(kernel, (Z, X, R, piece, block)), out_sh...]
where the time goes in v6:
time: 81.5 us; the launch traced here: 81.2 us
  Pallas kernels  79.8 us (98%)
  local copies, waits for them, and re-layouts  1.32 us (2%)
    pallas_call x1, Pallas kernels, body(): pl.pallas_call(functools.partial(kernel, (Z, X, R, piece, block)), out_sh...  79.8 us

profile of v6, /device:TPU:1, one launch (start us, length us, event | category | flops | bytes accessed | tf_op | source)
XLA Modules:
  0.0 81.2 jit_solution(16210856033141697029)
XLA Ops:
  0.0 79.8 %shard_map.91 = f32[1,16,256]{2,1,0:T(8,128)} custom-call(bf16[1,16,256]{2,1,0:T(8,128)(2,1)} %exc.1, f32[3,32768]{1,0:T(4,128)} %pts.1, f32[1,32768]{1,0:T(1,128)} %bitcast.7, s32[1,256]{1,0:T(1,128)} %bitcast.8, s32[1,256]{1,0:T(1,128)} %bitcast.9, s32[1,256]{1,0:T(1,128)} %bitcast.10, s32[2,4]{1,0:T(2,128)} %bitcast.11, bf16[1024,2048]{1,0:T(8,128)(2,1)} %bitcast.6, ...), custom_call_target="tpu_custom_call" | custom-call | tf_op jit(solution)/shard_map/pallas_call | solution.py:603
  79.8 1.3 %copy.11 = f32[1,16,256]{2,1,0:T(8,128)} copy(f32[1,16,256]{2,1,0:T(8,128)} %shard_map.91) | data formatting | bytes 32768

commit v7 on v6

--- a/solution.py
+++ b/solution.py
@@ -401,21 +401,13 @@
                 if kind == 0
                 else jnp.logical_not(is_last(k)) | (g == 1)
             )
-            for src in range(GROUPS * R):
-
-                @pl.when(takes & (src != me))
-                def _():
-                    remote(
-                        pbuf.at[k, kind, src],
-                        pbuf.at[k, kind, src],
-                        y_s.at[0, 0],
-                        y_r.at[k, kind, src],
-                        {"row": r},
-                    ).wait_recv()
-
             @pl.when(takes)
             def _():
                 pbuf[k, kind, me] = psend[k, kind, r]
+                for step in range(1, GROUPS * R):
+                    src = (me + step) % (GROUPS * R)
+                    landed = pbuf.at[k, kind, src]
+                    remote(landed, landed, y_s.at[0, 0], y_r.at[k, kind, src], {"row": r}).wait_recv()
                 total = pbuf[k, kind, 0]
                 for src in range(1, GROUPS * R):
                     total = total + pbuf[k, kind, src]
@@ -476,23 +468,19 @@
     collect(0)
 
     def iteration(k, carry):
+        shift = jnp.where(parity == g, 0, 1)
         for zi in range(Zh):
-            zs = GROUPS * zi + g
-
-            @pl.when(zs != z)
-            def _():
-                remote(
-                    tbuf.at[k, 0, zs], tbuf.at[k, 0, zs], t_s.at[0, 0], t_r.at[k, 0, zs], {"row": r}
-                ).wait_recv()
-
-        for zi in range(Zh):
-            zs = GROUPS * zi + g
-
-            @pl.when(zs != z)
-            def _():
-                remote(
-                    tbuf.at[k, 1, zs], tbuf.at[k, 1, zs], t_s.at[0, 0], t_r.at[k, 1, zs], {"row": r}
-                ).wait_recv()
+            zs = (z + GROUPS * zi + shift) % Z
+
+            def arrive(zs=zs):
+                for kind in (0, 1):
+                    landed = tbuf.at[k, kind, zs]
+                    remote(landed, landed, t_s.at[0, 0], t_r.at[k, kind, zs], {"row": r}).wait_recv()
+
+            if zi:
+                arrive()
+            else:
+                pl.when(shift != 0)(arrive)
 
         for zi in range(Zh):
             zs = GROUPS * zi + g
@@ -505,14 +493,19 @@
         for dx in x_order:
             we_copy(k, dx).start()
 
+        shift = jnp.where(parity == g, 1, 0)
         for zi in range(Zh):
-            zs = GROUPS * zi + (1 - g)
-
-            @pl.when(zs != z)
-            def _():
-                remote(
-                    tbuf.at[k, 1, zs], tbuf.at[k, 1, zs], t_s.at[0, 0], t_r.at[k, 1, zs], {"row": r}
-                ).wait_recv()
+            zs = (z + GROUPS * zi + shift) % Z
+
+            def arrive(zs=zs):
+                for kind in (1,):
+                    landed = tbuf.at[k, kind, zs]
+                    remote(landed, landed, t_s.at[0, 0], t_r.at[k, kind, zs], {"row": r}).wait_recv()
+
+            if zi:
+                arrive()
+            else:
+                pl.when(shift != 0)(arrive)
 
         sources = []
         for j in range(GROUPS):

time: 81.5 us -> 81.8 us (level)
  no operation moved by 1% of the time
where the time goes in v7:
time: 81.8 us; the launch traced here: 81.6 us
  Pallas kernels  80.3 us (98%)
  local copies, waits for them, and re-layouts  1.32 us (2%)
    pallas_call x1, Pallas kernels, body(): pl.pallas_call(functools.partial(kernel, (Z, X, R, piece, block)), out_sh...  80.3 us

profile of v7, /device:TPU:1, one launch (start us, length us, event | category | flops | bytes accessed | tf_op | source)
XLA Modules:
  0.0 81.6 jit_solution(4635682602111819149)
XLA Ops:
  0.0 80.3 %shard_map.91 = f32[1,16,256]{2,1,0:T(8,128)} custom-call(bf16[1,16,256]{2,1,0:T(8,128)(2,1)} %exc.1, f32[3,32768]{1,0:T(4,128)} %pts.1, f32[1,32768]{1,0:T(1,128)} %bitcast.7, s32[1,256]{1,0:T(1,128)} %bitcast.8, s32[1,256]{1,0:T(1,128)} %bitcast.9, s32[1,256]{1,0:T(1,128)} %bitcast.10, s32[2,4]{1,0:T(2,128)} %bitcast.11, bf16[1024,2048]{1,0:T(8,128)(2,1)} %bitcast.6, ...), custom_call_target="tpu_custom_call" | custom-call | tf_op jit(solution)/shard_map/pallas_call | solution.py:596
  80.3 1.3 %copy.11 = f32[1,16,256]{2,1,0:T(8,128)} copy(f32[1,16,256]{2,1,0:T(8,128)} %shard_map.91) | data formatting | bytes 32768
